TPU v7x, 256 devices: a whole 4x4x8 slice. The times are simulated.
256 devices in a mesh: dp: 16 (over z, core), seq: 16 (over y, x).
Axes of the slice: x: 4, y: 4, z: 8, core: 2. Of those that a mesh axis runs over, the one named last changes fastest.
Arguments:
- layer_in: bfloat16 [16, 2048, 2560], P('dp', 'seq'), may hold values from -6 to 6
- scan_in: bfloat16 [16, 2048, 2560], P('dp', 'seq'), may hold values from -6 to 6
- step_size: float32 [16, 2048, 40], P('dp', 'seq'), may hold values from 0.0024 to 0.041
- b_weight: bfloat16 [2560, 64], replicated, may hold values from -0.125 to 0.125
- c_weight: bfloat16 [2560, 64], replicated, may hold values from -0.125 to 0.125
- decay_rate: float32 [40], replicated, may hold values from 0.0005 to 10
- skip_gain: float32 [40], replicated, may hold values from 0.25 to 1.75
- out_grad: bfloat16 [16, 2048, 2560], P('dp', 'seq'), may hold values from -6 to 6
- doc_lengths: int32 [16, 4], P('dp'), may hold values from 1 to 1024, 2048 in all within a row
- block_order: int32 [16, 16], P('dp'), may hold values from 0 to 15, each once within a row
Outputs:
- scan_out: bfloat16 [16, 2048, 2560], P('dp', 'seq')
- b_weight_grad: float32 [2560, 64], replicated
- c_weight_grad: float32 [2560, 64], replicated
Inputs may be any that keep to these rules, and one draw needn't show every extreme that they name: `block_order`: each row holds 0 to 15 once each. `doc_lengths`: each row sums to 2048; its longest document has 1024 tokens.
All inputs are finite; a program needn't handle non-finite values.
Results may differ from a plain program's by a relative error of at most 0.0055.
Values sent between devices are 32-bit elements.
No kernel may reach another device: no remote copies, remote signals or barrier semaphores. Data moves between devices by JAX's collectives and lax.ppermute only.
A program may use at most 128 MiB of HBM per device.

v0:
```python
import math

import jax
import jax.numpy as jnp
from jax import lax
from jax.sharding import Mesh
from jax.sharding import PartitionSpec as P

SEQ = ("seq_0", "seq_1")
DP_SEQ = ("dp", "seq_0", "seq_1")


precise = lax.Precision.HIGHEST


def gathered_by_axis(array, axes, dim):
    for axis in reversed(axes):
        array = lax.all_gather(array, axis, axis=dim, tiled=True)
    return array


def side_by_side(arrays, axis, dim, along):
    both = jnp.concatenate(arrays, axis=along)
    whole, at, done = (lax.all_gather(both, axis, axis=dim, tiled=True), 0, [])
    for a in arrays:
        done.append(lax.slice_in_dim(whole, at, at + a.shape[along], axis=along))
        at += a.shape[along]
    return tuple(done)


def link_weights(low_block, high_block, totals):
    block_count = totals.shape[0]
    places = jnp.arange(block_count, dtype=jnp.int32)
    inside = (low_block[:, None] < places[None, :]) & (places[None, :] < high_block[:, None])
    factors = jnp.where(inside[:, :, None], totals[None, :, :], jnp.float32(1.0))
    return jnp.prod(factors, axis=1) * (low_block < high_block).astype(jnp.float32)[:, None]


def per_device(
    layer_in,
    scan_in,
    step_size,
    b_weight,
    c_weight,
    decay_rate,
    skip_gain,
    out_grad,
    doc_lengths,
    block_order,
):
    row_count = scan_in.shape[1]
    head_count = decay_rate.shape[0]
    head_width = scan_in.shape[2] // head_count
    state_count = b_weight.shape[1]
    block_count = lax.axis_size(SEQ)
    group_count = lax.axis_size("dp")
    my_slot = lax.axis_index(SEQ)
    tokens = layer_in[0]
    b_mat = jnp.dot(tokens, b_weight, preferred_element_type=jnp.float32).astype(jnp.bfloat16)
    c_mat = jnp.dot(tokens, c_weight, preferred_element_type=jnp.float32).astype(jnp.bfloat16)
    b_float = b_mat.astype(jnp.float32)
    c_float = c_mat.astype(jnp.float32)
    order_row = block_order[0]
    my_block = lax.dynamic_index_in_dim(order_row, my_slot, 0, keepdims=False)
    lengths = doc_lengths[0]
    doc_ends = jnp.cumsum(lengths, dtype=jnp.int32)
    doc_starts = doc_ends - lengths
    positions = my_block * row_count + jnp.arange(row_count, dtype=jnp.int32)
    segment = jnp.sum((doc_starts[None, :] <= positions[:, None]).astype(jnp.int32), axis=1)
    begins = jnp.any(doc_starts[None, :] == positions[:, None], axis=1)
    step_sizes = step_size[0]
    log_rates = -step_sizes * decay_rate[None, :]
    offsets = jnp.arange(row_count, dtype=jnp.int32)
    lower_tri = offsets[:, None] >= offsets[None, :]
    cumlog = jnp.dot(lower_tri.astype(jnp.float32), log_rates, precision=precise)
    linked = (segment == segment[0]) & jnp.logical_not(begins[0])
    in_last = segment == segment[row_count - 1]
    entering = jnp.where(linked[:, None], jnp.exp(cumlog), jnp.float32(0.0))
    leaving = jnp.where(
        in_last[:, None], jnp.exp(cumlog[row_count - 1][None, :] - cumlog), jnp.float32(0.0)
    )
    block_total = entering[row_count - 1]
    x_heads = scan_in[0].reshape(row_count, head_count, head_width)
    grad_heads = out_grad[0].reshape(row_count, head_count, head_width)
    driven = x_heads.astype(jnp.float32) * step_sizes[:, :, None]
    pushed = driven * leaving[:, :, None]
    seen = grad_heads.astype(jnp.float32) * entering[:, :, None]
    own_state = jnp.einsum("thp,tn->hpn", pushed, b_float, precision=precise).reshape(
        head_count, head_width * state_count
    )
    own_adjoint = jnp.einsum("thp,tn->hpn", seen, c_float, precision=precise).reshape(
        head_count, head_width * state_count
    )
    all_totals = gathered_by_axis(block_total[None, :], SEQ, 0)
    held_slots = jnp.arange(block_count, dtype=jnp.int32)
    onehot = (order_row[None, :] == held_slots[:, None]).astype(jnp.float32)
    seq_totals = jnp.dot(onehot, all_totals, precision=precise)
    mine_vector = jnp.full((block_count,), my_block, jnp.int32)
    from_earlier = link_weights(order_row, mine_vector, seq_totals)
    from_later = link_weights(mine_vector, order_row, seq_totals)
    pieces = side_by_side((own_state[None], own_adjoint[None]), SEQ, 0, 1)
    incoming = jnp.einsum("ch,chz->hz", from_earlier, pieces[0], precision=precise)
    returning = jnp.einsum("ch,chz->hz", from_later, pieces[1], precision=precise)
    incoming = incoming.reshape(head_count, head_width, state_count)
    returning = returning.reshape(head_count, head_width, state_count)
    scores = jnp.einsum("tn,sn->ts", c_mat, b_mat, preferred_element_type=jnp.float32)
    causal = lower_tri & (segment[:, None] == segment[None, :])
    set_size = math.gcd(head_count, 16)
    set_count = head_count // set_size

    def per_set(set_index, totals_pair):
        out_acc, mix_acc = totals_pair
        head_first = set_index * set_size
        set_log = lax.dynamic_slice_in_dim(cumlog, head_first, set_size, 1)
        set_steps = lax.dynamic_slice_in_dim(step_sizes, head_first, set_size, 1)
        set_driven = lax.dynamic_slice_in_dim(driven, head_first, set_size, 1)
        set_inputs = lax.dynamic_slice_in_dim(x_heads, head_first, set_size, 1)
        set_cotan = lax.dynamic_slice_in_dim(grad_heads, head_first, set_size, 1)
        log_gaps = set_log.T[:, :, None] - set_log.T[:, None, :]
        decays = jnp.exp(jnp.where(causal[None], log_gaps, jnp.float32(-1e30)))
        mixed = decays * scores[None]
        y_part = jnp.einsum("hts,shp->thp", mixed, set_driven, precision=precise)
        intersect = jnp.einsum(
            "thp,shp->hts", set_cotan, set_inputs, preferred_element_type=jnp.float32
        )
        q_part = jnp.sum(decays * intersect * set_steps.T[:, None, :], axis=0)
        out_acc = lax.dynamic_update_slice_in_dim(out_acc, y_part, head_first, 1)
        return (out_acc, mix_acc + q_part)

    start_pair = (
        jnp.zeros((row_count, head_count, head_width), jnp.float32),
        jnp.zeros((row_count, row_count), jnp.float32),
    )
    y_intra, mixing = lax.fori_loop(0, set_count, per_set, start_pair)
    y_cross = jnp.einsum("tn,hpn->thp", c_float, incoming, precision=precise) * entering[:, :, None]
    y_total = y_intra + y_cross + skip_gain[None, :, None] * x_heads.astype(jnp.float32)
    scan_out = y_total.reshape(row_count, head_count * head_width).astype(jnp.bfloat16)[None]
    grad_c = jnp.dot(mixing, b_float, precision=precise) + jnp.einsum(
        "thp,hpn->tn", seen, incoming, precision=precise
    )
    grad_b = jnp.einsum("ts,tn->sn", mixing, c_float, precision=precise) + jnp.einsum(
        "thp,hpn->tn", pushed, returning, precision=precise
    )
    local_b = jnp.einsum(
        "td,tn->dn", tokens, grad_b.astype(jnp.bfloat16), preferred_element_type=jnp.float32
    )
    local_c = jnp.einsum(
        "td,tn->dn", tokens, grad_c.astype(jnp.bfloat16), preferred_element_type=jnp.float32
    )
    summed_b, summed_c = lax.psum((local_b, local_c), DP_SEQ)
    scale = 1.0 / (group_count * row_count * block_count)
    return (scan_out, summed_b * scale, summed_c * scale)


def solution(mesh):
    split = Mesh(mesh.devices.reshape(mesh.shape["dp"], 4, 4), ("dp", "seq_0", "seq_1"))
    in_specs = (
        P("dp", SEQ, None),
        P("dp", SEQ, None),
        P("dp", SEQ, None),
        P(),
        P(),
        P(),
        P(),
        P("dp", SEQ, None),
        P("dp", None),
        P("dp", None),
    )
    out_specs = (P("dp", SEQ, None), P(), P())
    return jax.shard_map(
        per_device, mesh=split, in_specs=in_specs, out_specs=out_specs, check_vma=False
    )
```

profile of v0, /device:TPU:1, one launch (start us, length us, event | category | flops | bytes accessed | tf_op | source)
XLA Modules:
  0.0 487.6 jit_solution(7718597954793324110)
XLA Ops:
  7.3 1.3 constant_dynamic-slice_fusion
  9.3 0.8 reduce-window_clone.1
  10.1 0.7 subtract_bitcast_fusion
  10.9 0.6 fusion.51
  11.5 1.0 fusion.38
  12.7 1.4 copy.37
  14.5 1.3 broadcast_compare_fusion
  15.9 0.8 fusion.28
  16.7 1.3 broadcast_in_dim_reshape.6
  18.0 1.3 convolution_convert_fusion.1
  19.6 0.8 fusion.25
  20.4 1.3 broadcast_in_dim_reshape.7
  21.7 2.4 pad_maximum_fusion
  24.2 1.7 bitcast_multiply_fusion
  26.1 8.5 %all-gather = f32[4,1,40]{2,1,0:T(1,128)S(1)} all-gather(f32[1,1,40]{2,1,0:T(1,128)S(1)} %bitcast.114), channel_id=1, replica_groups=mesh['dp'=16,'seq_0'=4,'seq_1'=4] {'seq_1'}, dimensions={0}, use_global_device_ids=true | all-gather | bytes 800 | tf_op jit(solution)/shard_map/all_gather | solution.py:18
  34.6 8.8 %all-gather.1 = f32[4,4,40]{2,1,0:T(4,128)S(1)} all-gather(f32[1,4,40]{2,1,0:T(4,128)S(1)} %bitcast.111), channel_id=1, replica_groups=mesh['dp'=16,'seq_0'=4,'seq_1'=4] {'seq_0'}, dimensions={0}, use_global_device_ids=true | all-gather | bytes 3200 | tf_op jit(solution)/shard_map/all_gather | solution.py:18
  43.5 0.7 iota_compare_fusion.8
  44.2 0.7 compare_convert_fusion
  45.5 0.8 fusion.52
  46.3 1.3 convert_multiply_fusion.1
  47.7 13.3 %while.16 = (s32[]{:T(128)}, f32[128,40,64]{0,2,1:T(8,128)S(1)}, f32[128,128]{1,0:T(8,128)S(1)}, f32[128,40,64]{0,2,1:T(8,128)}, f32[128,40]{0,1:T(8,128)S(1)}, ...) while((s32[]{:T(128)}, f32[128,40,64]{0,2,1:T(8,128)S(1)}, ...), condition=%wide.region_4.5_spmd.clone, body=%wide.region_2.4_spmd.clone.sunk | while | flops 118554632 | bytes 1202881 | solution.py:134
  47.9 2.1 fusion.83
  50.0 0.3 fusion.84
  50.5 2.1 fusion.83
  52.7 0.3 fusion.84
  53.2 2.1 fusion.83
  55.3 0.3 fusion.84
  55.8 2.1 fusion.83
  58.0 0.3 fusion.84
  58.5 2.1 fusion.83
  60.6 0.3 fusion.84
  61.0 104.6 %all-gather.4.cloned.1.call-done = f32[16,80,4096]{2,1,0:T(8,128)} async-done(((f32[1,80,4096]{2,1,0:T(8,128)}), f32[16,80,4096]{2,1,0:T(8,128)}) %all-gather.4.cloned.1.call-update) | async-done | bytes 20971536 | tf_op jit(solution)/shard_map/all_gather | solution.py:24
  165.6 12.1 %fusion.50 = (f32[16,40,4096]{2,1,0:T(8,128)}, f32[16,40,4096]{2,1,0:T(8,128)S(1)}) fusion(f32[16,80,4096]{2,1,0:T(8,128)} %all-gather.4.cloned.1.call-done), kind=kLoop, calls=%fused_computation.98 | loop fusion | bytes 41943040 | tf_op jit(solution)/shard_map/slice | solution.py:26
  177.7 9.8 %fusion.20 = f32[40,1,4096]{2,1,0:T(1,128)S(1)} fusion(f32[16,40,1]{0,2,1:T(1,128)S(1)} %copy.44, f32[16,40,4096]{2,1,0:T(8,128)S(1)} %get-tuple-element.253), kind=kOutput, calls=%fused_computation.26 | convolution fusion | flops 31457280 | bytes 11143680 | tf_op jit(solution)/shard_map/ch,chz->hz/dot_general | solution.py:102
  187.5 0.4 copy.59
  187.9 0.5 reshape.147
  188.4 3.6 convolution_bitcast_fusion.3
  192.3 1.1 convolution_bitcast_fusion.1
  193.3 15.4 %fusion.18 = f32[40,1,4096]{2,1,0:T(1,128)S(1)} fusion(f32[16,40,1]{0,2,1:T(1,128)S(1)} %copy.47, f32[16,40,4096]{2,1,0:T(8,128)} %get-tuple-element.252), kind=kOutput, calls=%fused_computation.24 | convolution fusion | flops 31457280 | bytes 11143680 | tf_op jit(solution)/shard_map/ch,chz->hz/dot_general | solution.py:103
  208.7 1.2 copy.58
  209.9 2.7 reshape.148
  212.6 4.0 convolution_bitcast_fusion.4
  216.8 1.1 convolution_bitcast_fusion.2
  217.9 2.2 fusion.24
  220.1 1.1 copy.43
  221.2 256.7 %all-reduce.3.cloned.1.call-done = (f32[2560,64]{0,1:T(8,128)}, f32[2560,64]{0,1:T(8,128)}) async-done(((f32[2560,64]{0,1:T(8,128)}, f32[2560,64]{0,1:T(8,128)}), (f32[2560,64]{0,1:T(8,128)}, f32[2560,64]{0,1:T(8,128)})) %all-reduce.3.cloned.1.call-update) | async-done | bytes 1310736 | tf_op jit(solution)/shard_map/psum | solution.py:150
  477.9 2.0 broadcast_multiply_fusion
  479.9 0.9 broadcast_multiply_fusion.1
  (54 shorter events, 3.2 us)
Async XLA Ops:
  7.2 7.0 %copy-start = (bf16[1,128,2560]{2,1,0:T(8,128)(2,1)S(1)}, bf16[1,128,2560]{2,1,0:T(8,128)(2,1)}, u32[]{:S(2)}) copy-start(bf16[1,128,2560]{2,1,0:T(8,128)(2,1)} %param.12) | copy-start | bytes 1966084
  7.2 8.7 %copy-start.4 = (f32[1,128,40]{1,2,0:T(8,128)S(1)}, f32[1,128,40]{1,2,0:T(8,128)}, u32[]{:S(2)}) copy-start(f32[1,128,40]{1,2,0:T(8,128)} %param.14) | copy-start | bytes 61444
  7.2 6.9 %copy-start.5 = (bf16[2560,64]{0,1:T(8,128)(2,1)S(1)}, bf16[2560,64]{0,1:T(8,128)(2,1)}, u32[]{:S(2)}) copy-start(bf16[2560,64]{0,1:T(8,128)(2,1)} %param.15) | copy-start | bytes 983044
  7.2 158.4 %all-gather.4.cloned.1.call-start = ((), (), s32[]{:S(2)}) async-start(), calls=%async_computation | async-start | bytes 22282240 | tf_op jit(solution)/shard_map/all_gather | solution.py:24
  16.7 2.6 copy-start.2
  24.2 20.0 %copy-start.6 = (s32[1,16]{1,0:T(1,128)S(1)}, s32[1,16]{1,0:T(1,128)}, u32[]{:S(2)}) copy-start(s32[1,16]{1,0:T(1,128)} %param.21) | copy-start | bytes 196
  24.2 453.7 %all-reduce.3.cloned.1.call-start = ((), (), s32[]{:S(2)}) async-start(), calls=%async_computation.1 | async-start | bytes 2621440 | tf_op jit(solution)/shard_map/psum | solution.py:150
  61.0 116.7 %copy-start.1 = (f32[128,40,64]{0,2,1:T(8,128)}, f32[128,40,64]{0,2,1:T(8,128)S(1)}, u32[]{:S(2)}) copy-start(f32[128,40,64]{0,2,1:T(8,128)S(1)} %get-tuple-element.173) | copy-start | bytes 3932164
  216.8 1.1 copy-start.7
  477.9 2.0 copy-start.3
Sparse Core Ops, SparseCore 0:
  24.3 141.2 all-gather.3
  218.1 259.7 all-reduce.2
where the time goes:
time: 489 us; the launch traced here: 488 us
  waiting for transfers between devices  361 us (74%)
  matrix products  55.1 us (11%)
  local copies, waits for them, and re-layouts  24.9 us (5%)
  blocking collectives  17.4 us (4%)
  between operations  15 us (3%)
  other arithmetic  13.6 us (3%)
    psum x1, waiting for transfers between devices, per_device(): summed_b, summed_c = lax.psum((local_b, local_c), DP_SEQ)  257 us
    all_gather x1, waiting for transfers between devices, side_by_side(): whole, at, done = (lax.all_gather(both, axis, axis=dim, tiled=True), 0, [])  105 us
    all_gather x2, blocking collectives, gathered_by_axis(): array = lax.all_gather(array, axis, axis=dim, tiled=True)  17.4 us
    dot_general x1, matrix products, per_device(): jnp.einsum('ch,chz->hz', from_later, pieces[1], precision=precise)  15.4 us
    slice x1, local copies, waits for them, and re-layouts, side_by_side(): done.append(lax.slice_in_dim(whole, at, at + a.shape[along], axis=along))  12.1 us
    dot_general x5, matrix products, per_set(): y_part = jnp.einsum('hts,shp->thp', mixed, set_driven, precision=precise)  10.7 us
    dot_general x1, matrix products, per_device(): jnp.einsum('ch,chz->hz', from_earlier, pieces[0], precision=precise)  9.78 us
  transfers between devices with their start and end apart: 2, of which 2 were waited for; matrix products, arithmetic and copies ran while one was open for 5% of the time, Pallas kernels for 0%

commit v1 on v0

v1 whole, which is shorter than its diff:
```python
import functools

import jax
import jax.numpy as jnp
from jax import lax
from jax.experimental import pallas as pl
from jax.experimental.pallas import tpu as pltpu
from jax.sharding import Mesh
from jax.sharding import PartitionSpec as P

SEQ = ("y", "x")
DP = ("z", "core")
F32 = jnp.float32
BF16 = jnp.bfloat16
CHUNK = 256
EXTRA = 128

VMEM = pl.BlockSpec(memory_space=pltpu.VMEM)
HBM = pl.BlockSpec(memory_space=pltpu.HBM)
SMEM = pl.BlockSpec(memory_space=pltpu.SMEM)
ALL_VMEM = pltpu.CompilerParams(vmem_limit_bytes=67043328)
PARAMS = pltpu.CompilerParams(vmem_limit_bytes=48 * 1024 * 1024)


def dot(a, b, dims=((1,), (0,))):
    return lax.dot_general(a, b, (dims, ((), ())), preferred_element_type=F32)


def dot_nt(a, b):
    return dot(a, b, ((1,), (1,)))


def dot_tn(a, b):
    return dot(a, b, ((0,), (0,)))


def slot_index():
    return lax.axis_index("y") * lax.axis_size("x") + lax.axis_index("x")


def spread(values, first, count, width):
    rows = values.shape[0]
    per = 128 // width
    lane = lax.broadcasted_iota(jnp.int32, (rows, 128), 1)
    parts = []
    for j in range(0, count, per):
        piece = jnp.broadcast_to(values[:, first + j : first + j + 1], (rows, 128))
        for k in range(1, per):
            other = jnp.broadcast_to(values[:, first + j + k : first + j + k + 1], (rows, 128))
            piece = jnp.where(lane >= k * width, other, piece)
        parts.append(piece)
    return jnp.concatenate(parts, axis=1) if len(parts) > 1 else parts[0]


def count_started(starts, position):
    return sum((start <= position).astype(jnp.int32) for start in starts)


def states_kernel(
    lengths_hbm, order_hbm, layer_hbm, x_hbm, grad_hbm, step_hbm, bw_hbm, cw_hbm, rate_hbm, gain_hbm,
    send_ref, layer_ref, x_ref, pushed_ref, seen_ref, b_ref, c_ref, c_linked_ref, scores_ref,
    causal_ref, linked_ref, last_ref, enter_ref, total_ref, gain_ref,
    lengths_ref, order_ref, grad_ref, step_ref, bw_ref, cw_ref, rate_ref, sems,
):
    pairs = (
        (lengths_hbm, lengths_ref), (order_hbm, order_ref), (rate_hbm, rate_ref),
        (step_hbm, step_ref), (bw_hbm, bw_ref), (cw_hbm, cw_ref), (layer_hbm, layer_ref),
        (x_hbm, x_ref), (grad_hbm, grad_ref), (gain_hbm, gain_ref),
    )
    copies = [pltpu.make_async_copy(a, b, sems.at[i]) for i, (a, b) in enumerate(pairs)]
    for copy in copies:
        copy.start()
    rows, inner = x_ref.shape[1:]
    heads = rate_ref.shape[1]
    width = inner // heads
    docs = lengths_ref.shape[1]
    blocks = send_ref.shape[0]
    half = blocks // 2
    state = bw_ref.shape[0]
    for copy in copies[:4]:
        copy.wait()
    first = order_ref[0, slot_index()] * rows
    starts = [jnp.int32(0)]
    for j in range(docs - 1):
        starts.append(starts[-1] + lengths_ref[0, j])
    across = (rows, rows)
    at_row = lax.broadcasted_iota(jnp.int32, across, 0)
    at_column = lax.broadcasted_iota(jnp.int32, across, 1)
    column = count_started(starts, first + at_row)
    row = count_started(starts, first + at_column)
    before = count_started(starts, first - 1)
    last = count_started(starts, first + rows - 1)
    tri = at_row >= at_column
    causal = tri & (column == row)
    linked = column[:, :state] == before
    in_last = column[:, :state] == last
    causal_ref[...] = causal.astype(F32)
    linked_ref[...] = linked.astype(F32)
    last_ref[...] = in_last.astype(F32)
    steps = step_ref[0].T
    logs = -(steps * rate_ref[...])
    cum = lax.dot_general(
        tri.astype(F32), logs, (((1,), (0,)), ((), ())),
        precision=lax.Precision.HIGHEST, preferred_element_type=F32,
    )
    enter = jnp.exp(cum)
    leave = steps * jnp.exp(-cum)
    enter_ref[...] = enter
    whole = enter[rows - 1 :, :]
    total_ref[...] = whole
    total = whole * (before == last).astype(F32)
    send_ref[:, :, inner : inner + heads] = jnp.broadcast_to(total[None], (blocks, 8, heads))
    for copy in copies[4:7]:
        copy.wait()
    tokens = layer_ref[0]
    b_mat = dot_nt(tokens, bw_ref[...]).astype(BF16)
    c_mat = dot_nt(tokens, cw_ref[...]).astype(BF16)
    b_ref[...] = b_mat
    c_ref[...] = c_mat
    scores_ref[...] = jnp.where(causal, dot_nt(c_mat, b_mat), 0.0).astype(BF16)
    b_last = jnp.where(in_last, b_mat.astype(F32), 0.0).astype(BF16)
    c_linked = jnp.where(linked, c_mat.astype(F32), 0.0).astype(BF16)
    c_linked_ref[...] = c_linked
    for copy in copies[7:]:
        copy.wait()
    per = CHUNK // width
    for at in range(0, inner, CHUNK):
        cols = slice(at, at + CHUNK)
        h = at // width
        pushed = (spread(leave, h, per, width) * x_ref[0, :, cols].astype(F32)).astype(BF16)
        seen = (spread(enter, h, per, width) * grad_ref[0, :, cols].astype(F32)).astype(BF16)
        pushed_ref[:, cols] = pushed
        seen_ref[:, cols] = seen
        own = dot_tn(b_last, pushed) * spread(whole, h, per, width)
        adj = dot_tn(c_linked, seen)
        send_ref[:half, :, cols] = own.reshape(half, 8, CHUNK)
        send_ref[half:, :, cols] = adj.reshape(half, 8, CHUNK)


def chain_kernel(order_ref, got_ref, out_ref, held_ref):
    blocks, _, inner = out_ref.shape
    heads = inner // 64
    for slot in range(blocks):
        held_ref[order_ref[0, slot]] = jnp.int32(slot)
    backward = slot_index() >= blocks // 2
    carry = jnp.zeros(out_ref.shape[1:], F32)
    for k in range(blocks):
        slot = held_ref[jnp.where(backward, blocks - 1 - k, k)]
        out_ref[slot] = carry
        if k < blocks - 1:
            totals = got_ref[slot, :, inner : inner + heads]
            carry = carry * spread(totals, 0, heads, 64) + got_ref[slot, :, :inner]


def grads_kernel(
    layer_ref, got_ref, pushed_ref, seen_ref, b_ref, c_ref, causal_ref, linked_ref, last_ref,
    total_ref,
    came_ref, keep_ref, give_ref, ret_ref,
):
    rows, inner = pushed_ref.shape
    heads = total_ref.shape[1]
    width = inner // heads
    blocks = got_ref.shape[0]
    half = blocks // 2
    state = b_ref.shape[1]
    whole = total_ref[...]
    per = CHUNK // width
    for at in range(0, inner, CHUNK):
        cols = slice(at, at + CHUNK)
        back = got_ref[half:, :, cols].reshape(state, CHUNK)
        came_ref[:, cols] = got_ref[:half, :, cols].reshape(state, CHUNK).astype(BF16)
        ret_ref[:, cols] = (back * spread(whole, at // width, per, width)).astype(BF16)
    pushed = pushed_ref[...]
    seen = seen_ref[...]
    mixing = jnp.where(causal_ref[...] > 0.5, dot_nt(seen, pushed), 0.0).astype(BF16)
    linked = linked_ref[...] > 0.5
    in_last = last_ref[...] > 0.5
    d_c = dot(mixing, b_ref[...]) + jnp.where(linked, dot_nt(seen, came_ref[...]), 0.0)
    d_b = dot_tn(mixing, c_ref[...]) + jnp.where(in_last, dot_nt(pushed, ret_ref[...]), 0.0)
    scale = 1.0 / (rows * blocks * lax.axis_size("z") * lax.axis_size("core"))
    first = lax.axis_index("core") == 0
    mine = jnp.where(first, d_b, d_c).astype(BF16)
    other = jnp.where(first, d_c, d_b).astype(BF16)
    columns = layer_ref.shape[2] // 128
    for at in range(0, layer_ref.shape[2], CHUNK):
        tokens = layer_ref[0, :, at : at + CHUNK]
        for side, to_ref in ((other, give_ref), (mine, keep_ref)):
            part = dot_tn(side, tokens) * scale
            for r in range(state // 8):
                for c in range(CHUNK // 128):
                    tile = r * columns + at // 128 + c
                    to_ref[tile] = part[8 * r : 8 * r + 8, 128 * c : 128 * c + 128]


def output_kernel(x_ref, gain_ref, came_ref, pushed_ref, scores_ref, c_linked_ref, enter_ref, out_ref):
    _, inner = pushed_ref.shape
    heads = gain_ref.shape[1]
    width = inner // heads
    scores = scores_ref[...]
    c_linked = c_linked_ref[...]
    enter = enter_ref[...]
    gain = gain_ref[...]
    per = CHUNK // width
    for at in range(0, inner, CHUNK):
        cols = slice(at, at + CHUNK)
        h = at // width
        mixed = dot(scores, pushed_ref[:, cols]) + dot(c_linked, came_ref[:, cols])
        skip = spread(gain, h, per, width) * x_ref[0, :, cols].astype(F32)
        out_ref[0, :, cols] = (spread(enter, h, per, width) * mixed + skip).astype(BF16)


def unpack_kernel(mine_ref, other_ref, b_ref, c_ref):
    columns = b_ref.shape[1] // 128

    def write(from_ref, to_ref):
        for r in range(to_ref.shape[0] // 8):
            for c in range(columns):
                to_ref[8 * r : 8 * r + 8, 128 * c : 128 * c + 128] = from_ref[r * columns + c]

    first = lax.axis_index("core") == 0

    @pl.when(first)
    def _():
        write(mine_ref, b_ref)
        write(other_ref, c_ref)

    @pl.when(jnp.logical_not(first))
    def _():
        write(other_ref, b_ref)
        write(mine_ref, c_ref)


def shape(*dims, dtype=F32):
    return jax.ShapeDtypeStruct(dims, dtype)


def swap_cores(a):
    return lax.ppermute(a, "core", [(0, 1), (1, 0)])


def exchange(a, axes):
    return lax.all_to_all(a, axes, 0, 0, tiled=True)


def everywhere(a, axes):
    return exchange(jnp.broadcast_to(a[None], (lax.axis_size(axes),) + a.shape), axes)


def per_device(
    layer_in, scan_in, step_size, b_weight, c_weight, decay_rate, skip_gain, out_grad, doc_lengths,
    block_order,
):
    _, rows, inner = scan_in.shape
    width_in, state = b_weight.shape
    tile_cols = width_in // 128
    heads = decay_rate.shape[0]
    blocks = lax.axis_size(SEQ)
    docs = doc_lengths.shape[1]
    states = pl.pallas_call(
        states_kernel,
        out_shape=(
            shape(blocks, 8, inner + EXTRA),
            shape(1, rows, width_in, dtype=BF16),
            shape(1, rows, inner, dtype=BF16),
            shape(rows, inner, dtype=BF16),
            shape(rows, inner, dtype=BF16),
            shape(rows, state, dtype=BF16),
            shape(rows, state, dtype=BF16),
            shape(rows, state, dtype=BF16),
            shape(rows, rows, dtype=BF16),
            shape(rows, rows),
            shape(rows, state),
            shape(rows, state),
            shape(rows, heads),
            shape(1, heads),
            shape(1, heads),
        ),
        in_specs=[HBM] * 10,
        out_specs=(VMEM,) * 15,
        scratch_shapes=[
            pltpu.SMEM((1, docs), jnp.int32),
            pltpu.SMEM((1, blocks), jnp.int32),
            pltpu.VMEM((1, rows, inner), BF16),
            pltpu.VMEM((1, heads, rows), F32),
            pltpu.VMEM((state, width_in), BF16),
            pltpu.VMEM((state, width_in), BF16),
            pltpu.VMEM((1, heads), F32),
            pltpu.SemaphoreType.DMA((10,)),
        ],
        compiler_params=ALL_VMEM,
    )(
        doc_lengths, block_order, layer_in, scan_in, out_grad, jnp.swapaxes(step_size, 1, 2),
        b_weight.T, c_weight.T, decay_rate[None], skip_gain[None],
    )
    send, layer, x, pushed, seen, b_mat, c_mat, c_linked, scores, causal, linked, in_last = states[:12]
    enter, total, gain = states[12:]
    got = exchange(send, SEQ)
    carried = pl.pallas_call(
        chain_kernel,
        out_shape=shape(blocks, 8, inner),
        in_specs=[SMEM, VMEM],
        out_specs=VMEM,
        scratch_shapes=[pltpu.SMEM((blocks,), jnp.int32)],
        compiler_params=PARAMS,
    )(block_order, got)
    back = exchange(carried, SEQ)
    came, keep, give = pl.pallas_call(
        grads_kernel,
        out_shape=(
            shape(state, inner, dtype=BF16),
            shape(state // 8 * tile_cols, 8, 128),
            shape(state // 8 * tile_cols, 8, 128),
        ),
        in_specs=[VMEM] * 10,
        out_specs=(VMEM,) * 3,
        scratch_shapes=[pltpu.VMEM((state, inner), BF16)],
        compiler_params=PARAMS,
        cost_estimate=pl.CostEstimate(flops=10**9, bytes_accessed=10**6, transcendentals=0),
    )(layer, back, pushed, seen, b_mat, c_mat, causal, linked, in_last, total)
    scan_out = pl.pallas_call(
        output_kernel,
        out_shape=shape(1, rows, inner, dtype=BF16),
        in_specs=[VMEM] * 7,
        out_specs=VMEM,
        compiler_params=PARAMS,
        cost_estimate=pl.CostEstimate(flops=10**9, bytes_accessed=10**6, transcendentals=0),
    )(x, gain, came, pushed, scores, c_linked, enter)
    local = keep + swap_cores(give)
    tiles = local.shape[0] // blocks
    share = jnp.sum(exchange(local.reshape(blocks, tiles, 8, 128), SEQ), axis=0)
    share = jnp.sum(everywhere(share, "z"), axis=0)
    mine = everywhere(share, SEQ).reshape(local.shape)
    other = swap_cores(mine)
    b_grad, c_grad = pl.pallas_call(
        unpack_kernel,
        out_shape=(shape(state, width_in), shape(state, width_in)),
        in_specs=[VMEM] * 2,
        out_specs=(VMEM,) * 2,
        compiler_params=PARAMS,
    )(mine, other)
    return scan_out, b_grad.T, c_grad.T


def solution(mesh):
    seq = mesh.shape["seq"]
    side = 4 if seq % 4 == 0 else 1
    split = Mesh(
        mesh.devices.reshape(mesh.shape["dp"] // 2, 2, seq // side, side), ("z", "core", "y", "x")
    )
    rows = P(DP, SEQ, None)
    group = P(DP, None)
    in_specs = (rows, rows, rows, P(), P(), P(), P(), rows, group, group)
    return jax.shard_map(
        per_device, mesh=split, in_specs=in_specs, out_specs=(rows, P(), P()), check_vma=False
    )
```

time: 489 us -> 118 us (0.24)
  waiting for transfers between devices: 361 us -> 1.73 us
  blocking collectives: 17.4 us -> 96.9 us
  matrix products: 55.1 us -> 0 us
  local copies, waits for them, and re-layouts: 24.9 us -> 0.14 us
  between operations: 15 us -> 0.86 us
  other arithmetic: 13.6 us -> 0.13 us
  Pallas kernels: 0 us -> 11.2 us
  starting transfers between devices: 0.08 us -> 6.46 us
    psum x1 -> x0, waiting for transfers between devices: 257 us -> none  [per_device(): summed_b, summed_c = lax.psum((local_b, local_c), DP_SEQ)]
    all_gather x1 -> x0, waiting for transfers between devices: 105 us -> none  [side_by_side(): whole, at, done = (lax.all_gather(both, axis, axis=dim, tiled=True), 0, [])]
    all_to_all x0 -> x5, blocking collectives: none -> 96.9 us  [exchange(): return lax.all_to_all(a, axes, 0, 0, tiled=True)]
    dot_general x26 -> x0, matrix products: 55.1 us -> none  [the longest x1 15.4 us: per_device(): jnp.einsum('ch,chz->hz', from_later, pieces[1], precision=precise)]
    all_gather x2 -> x0, blocking collectives: 17.4 us -> none  [gathered_by_axis(): array = lax.all_gather(array, axis, axis=dim, tiled=True)]
    slice x4 -> x0, local copies, waits for them, and re-layouts: 13.1 us -> none  [the longest x1 12.1 us: side_by_side(): done.append(lax.slice_in_dim(whole, at, at + a.shape[along], axis=along))]
    pallas_call x0 -> x5, Pallas kernels: none -> 11.2 us  [the longest x1 5.25 us: per_device(): pl.pallas_call(states_kernel, out_shape=(shape(blocks, 8, inner + EXTRA),...]
    ppermute x0 -> x2, starting transfers between devices: none -> 6.46 us  [swap_cores(): return lax.ppermute(a, 'core', [(0, 1), (1, 0)])]
  transfers between devices with their start and end apart: 2 -> 2, of which waited for: 2 -> 1; matrix products, arithmetic and copies ran while one was open for 5% -> 0% of each run, Pallas kernels for 0% -> 1%
where the time goes in v1:
time: 118 us; the launch traced here: 117 us
  blocking collectives  96.9 us (82%)
  Pallas kernels  11.2 us (9%)
  starting transfers between devices  6.46 us (5%)
  waiting for transfers between devices  1.73 us (1%)
    all_to_all x5, blocking collectives, exchange(): return lax.all_to_all(a, axes, 0, 0, tiled=True)  96.9 us
    ppermute x2, starting transfers between devices, swap_cores(): return lax.ppermute(a, 'core', [(0, 1), (1, 0)])  6.46 us
    pallas_call x1, Pallas kernels, per_device(): pl.pallas_call(states_kernel, out_shape=(shape(blocks, 8, inner + EXTRA),...  5.25 us
  transfers between devices with their start and end apart: 2, of which 1 were waited for; matrix products, arithmetic and copies ran while one was open for 0% of the time, Pallas kernels for 1%

profile of v1, /device:TPU:1, one launch (start us, length us, event | category | flops | bytes accessed | tf_op | source)
XLA Modules:
  0.0 117.4 jit_solution(2634983303626673002)
XLA Ops:
  0.6 5.3 %shard_map.121 = (f32[16,8,2688]{2,1,0:T(8,128)}, bf16[1,128,2560]{2,1,0:T(8,128)(2,1)}, bf16[1,128,2560]{2,1,0:T(8,128)(2,1)}, bf16[128,2560]{1,0:T(8,128)(2,1)...) custom-call(s32[1,4]{1,0:T(1,128)} %lengths_hbm.1, ...), custom_call_target="tpu_custom_call" | custom-call | tf_op jit(solution)/shard_map/pallas_call | solution.py:259
  5.9 0.0 copy-start
  5.9 27.4 %all_to_all.25.got_ref = f32[16,8,2688]{2,1,0:T(8,128)S(1)} all-to-all(f32[16,8,2688]{2,1,0:T(8,128)} %get-tuple-element.26), channel_id=1, replica_groups=mesh['z'=8,'core'=2,'y'=4,'x'=4] {'y','x'}, dimensions={0} | all-to-all | bytes 2752512 | tf_op jit(solution)/shard_map/all_to_all | solution.py:242
  33.3 0.0 copy-done
  33.3 1.7 %shard_map.122 = f32[16,8,2560]{2,1,0:T(8,128)S(1)} custom-call(s32[1,16]{1,0:T(1,128)S(1)} %copy-done, f32[16,8,2688]{2,1,0:T(8,128)S(1)} %all_to_all.25.got_ref), custom_call_target="tpu_custom_call" | custom-call | tf_op jit(solution)/shard_map/pallas_call | solution.py:298
  35.1 0.0 copy-start.2
  35.1 0.0 copy-start.3
  35.1 0.0 copy-start.4
  35.1 0.0 copy-start.6
  35.1 0.0 copy-start.7
  35.1 0.0 copy-start.8
  35.1 0.0 copy-start.11
  35.1 0.0 copy-start.12
  35.1 0.0 copy-start.14
  35.2 21.6 %all_to_all.26.got_ref = f32[16,8,2560]{2,1,0:T(8,128)S(1)} all-to-all(f32[16,8,2560]{2,1,0:T(8,128)S(1)} %shard_map.122), channel_id=1, replica_groups=mesh['z'=8,'core'=2,'y'=4,'x'=4] {'y','x'}, dimensions={0} | all-to-all | bytes 2621440 | tf_op jit(solution)/shard_map/all_to_all | solution.py:242
  56.7 0.0 copy-done.2
  56.7 0.0 copy-done.3
  56.7 0.0 copy-done.4
  56.7 0.0 copy-done.6
  56.8 0.0 copy-done.7
  56.8 0.0 copy-done.8
  56.8 0.0 copy-done.11
  56.8 0.0 copy-done.12
  56.8 0.0 copy-done.14
  56.8 1.3 %shard_map.123 = (bf16[64,2560]{1,0:T(8,128)(2,1)S(1)}, f32[160,8,128]{2,1,0:T(8,128)S(1)}, f32[160,8,128]{2,1,0:T(8,128)S(1)}) custom-call(bf16[1,128,2560]{2,1,0:T(8,128)(2,1)S(1)} %copy-done.3, f32[16,8,2560]{2,1,0:T(8,128)S(1)} %all_to_all.26.got_ref, bf16[128,2560]{1,0:T(8,128)(2,1)S(1)} %copy-done.2, bf16[128,2560]{1,0:T(8,128)(2,1)S(1)} %copy-done.4, ...), custom_call_target="tpu_custom_call" | custom-call | flops 1000000000 | bytes 1000000 | tf_op jit(solution)/shard_map/pallas_call | solution.py:307
  58.2 2.6 %collective-permute-start = (f32[160,8,128]{2,1,0:T(8,128)S(1)}, f32[160,8,128]{2,1,0:T(8,128)S(1)}, u32[]{:S(2)}, u32[]{:S(2)}) collective-permute-start(f32[160,8,128]{2,1,0:T(8,128)S(1)} %get-tuple-element.40), channel_id=1, source_target_pairs={{0,16},{16,0},{1,17},{17,1},{2,18},{18,2},{3,19},{19,3},{4,20},{20... | collective-permute-start | bytes 1966088 | tf_op jit(solution)/shard_map/ppermute | solution.py:238
  60.8 1.7 %collective-permute-done = f32[160,8,128]{2,1,0:T(8,128)S(1)} collective-permute-done((f32[160,8,128]{2,1,0:T(8,128)S(1)}, f32[160,8,128]{2,1,0:T(8,128)S(1)}, u32[]{:S(2)}, u32[]{:S(2)}) %collective-permute-start) | collective-permute-done | bytes 655392 | tf_op jit(solution)/shard_map/ppermute | solution.py:238
  62.5 0.1 add.3
  62.6 15.1 %all_to_all.27 = f32[16,10,8,128]{3,2,1,0:T(8,128)S(1)} all-to-all(f32[16,10,8,128]{3,2,1,0:T(8,128)S(1)} %bitcast.11), channel_id=1, replica_groups=mesh['z'=8,'core'=2,'y'=4,'x'=4] {'y','x'}, dimensions={0} | all-to-all | bytes 1310720 | tf_op jit(solution)/shard_map/all_to_all | solution.py:242
  77.8 0.0 copy-start.1
  77.8 0.0 copy-start.5
  77.8 0.0 copy-start.9
  77.8 0.0 copy-start.10
  77.8 0.0 copy-start.13
  77.8 18.9 %all_to_all.28 = f32[8,10,8,128]{3,2,1,0:T(8,128)S(1)} all-to-all(f32[8,10,8,128]{3,2,1,0:T(8,128)S(1)} %broadcast_in_dim.20), channel_id=1, replica_groups=mesh['z'=8,'core'=2,'y'=4,'x'=4] {'z'}, dimensions={0} | all-to-all | bytes 655360 | tf_op jit(solution)/shard_map/all_to_all | solution.py:242
  96.8 13.9 %all_to_all.29 = f32[16,10,8,128]{3,2,1,0:T(8,128)S(1)} all-to-all(f32[16,10,8,128]{3,2,1,0:T(8,128)S(1)} %broadcast_in_dim.21), channel_id=1, replica_groups=mesh['z'=8,'core'=2,'y'=4,'x'=4] {'y','x'}, dimensions={0} | all-to-all | bytes 1310720 | tf_op jit(solution)/shard_map/all_to_all | solution.py:242
  110.7 3.8 %collective-permute-start.1 = (f32[160,8,128]{2,1,0:T(8,128)S(1)}, f32[160,8,128]{2,1,0:T(8,128)S(1)}, u32[]{:S(2)}, u32[]{:S(2)}) collective-permute-start(f32[160,8,128]{2,1,0:T(8,128)S(1)} %bitcast.9), channel_id=1, source_target_pairs={{0,16},{16,0},{1,17},{17,1},{2,18},{18,2},{3,19},{19,3},{4,20},{20... | collective-permute-start | bytes 1966088 | tf_op jit(solution)/shard_map/ppermute | solution.py:238
  114.5 0.0 copy-done.1
  114.5 0.0 copy-done.5
  114.5 0.0 copy-done.9
  114.5 0.0 copy-done.10
  114.5 0.0 copy-done.13
  114.5 1.8 %shard_map.124 = bf16[1,128,2560]{2,1,0:T(8,128)(2,1)} custom-call(bf16[1,128,2560]{2,1,0:T(8,128)(2,1)S(1)} %copy-done.1, f32[1,40]{1,0:T(1,128)S(1)} %copy-done.13, bf16[64,2560]{1,0:T(8,128)(2,1)S(1)} %get-tuple-element.35.came_ref, bf16[128,2560]{1,0:T(8,128)(2,1)S(1)} %copy-done.2, bf16[128,128]{1,0:T(8,128)(2,1)S(1)} %copy-done.10, ...), custom_call_target="tpu_custom_call" | custom-call | flops 1000000000 | bytes 1000000 | tf_op jit(solution)/shard_map/pallas_call | solution.py:320
  116.3 0.0 collective-permute-done.1.other_ref
  116.3 1.1 shard_map.125
  (4 shorter events, 0.1 us)
Async XLA Ops:
  5.9 27.4 %copy-start = (s32[1,16]{1,0:T(1,128)S(1)}, s32[1,16]{1,0:T(1,128)}, u32[]{:S(2)}) copy-start(s32[1,16]{1,0:T(1,128)} %order_ref.1) | copy-start | bytes 196
  35.1 21.7 %copy-start.2 = (bf16[128,2560]{1,0:T(8,128)(2,1)S(1)}, bf16[128,2560]{1,0:T(8,128)(2,1)}, u32[]{:S(2)}) copy-start(bf16[128,2560]{1,0:T(8,128)(2,1)} %get-tuple-element.27.pushed_ref) | copy-start | bytes 1966084
  35.1 21.7 %copy-start.3 = (bf16[1,128,2560]{2,1,0:T(8,128)(2,1)S(1)}, bf16[1,128,2560]{2,1,0:T(8,128)(2,1)}, u32[]{:S(2)}) copy-start(bf16[1,128,2560]{2,1,0:T(8,128)(2,1)} %get-tuple-element.25.layer_ref) | copy-start | bytes 1966084
  35.1 21.7 %copy-start.4 = (bf16[128,2560]{1,0:T(8,128)(2,1)S(1)}, bf16[128,2560]{1,0:T(8,128)(2,1)}, u32[]{:S(2)}) copy-start(bf16[128,2560]{1,0:T(8,128)(2,1)} %get-tuple-element.28.seen_ref) | copy-start | bytes 1966084
  35.1 21.7 %copy-start.6 = (f32[128,128]{1,0:T(8,128)S(1)}, f32[128,128]{1,0:T(8,128)}, u32[]{:S(2)}) copy-start(f32[128,128]{1,0:T(8,128)} %get-tuple-element.31.causal_ref) | copy-start | bytes 196612
  35.1 21.7 %copy-start.7 = (f32[128,64]{1,0:T(8,128)S(1)}, f32[128,64]{1,0:T(8,128)}, u32[]{:S(2)}) copy-start(f32[128,64]{1,0:T(8,128)} %get-tuple-element.32.linked_ref) | copy-start | bytes 98308
  35.1 21.7 %copy-start.8 = (f32[128,64]{1,0:T(8,128)S(1)}, f32[128,64]{1,0:T(8,128)}, u32[]{:S(2)}) copy-start(f32[128,64]{1,0:T(8,128)} %get-tuple-element.33.last_ref) | copy-start | bytes 98308
  35.1 21.7 %copy-start.11 = (bf16[128,64]{1,0:T(8,128)(2,1)S(1)}, bf16[128,64]{1,0:T(8,128)(2,1)}, u32[]{:S(2)}) copy-start(bf16[128,64]{1,0:T(8,128)(2,1)} %get-tuple-element.29.b_ref) | copy-start | bytes 49156
  35.1 21.7 %copy-start.12 = (bf16[128,64]{1,0:T(8,128)(2,1)S(1)}, bf16[128,64]{1,0:T(8,128)(2,1)}, u32[]{:S(2)}) copy-start(bf16[128,64]{1,0:T(8,128)(2,1)} %get-tuple-element.30.c_ref) | copy-start | bytes 49156
  35.1 21.7 %copy-start.14 = (f32[1,40]{1,0:T(1,128)S(1)}, f32[1,40]{1,0:T(1,128)}, u32[]{:S(2)}) copy-start(f32[1,40]{1,0:T(1,128)} %get-tuple-element.34.total_ref) | copy-start | bytes 484
  58.2 4.4 %collective-permute-start = (f32[160,8,128]{2,1,0:T(8,128)S(1)}, f32[160,8,128]{2,1,0:T(8,128)S(1)}, u32[]{:S(2)}, u32[]{:S(2)}) collective-permute-start(f32[160,8,128]{2,1,0:T(8,128)S(1)} %get-tuple-element.40), channel_id=1, source_target_pairs={{0,16},{16,0},{1,17},{17,1},{2,18},{18,2},{3,19},{19,3},{4,20},{20... | collective-permute-start | bytes 1966088 | tf_op jit(solution)/shard_map/ppermute | solution.py:238
  77.8 36.7 %copy-start.1 = (bf16[1,128,2560]{2,1,0:T(8,128)(2,1)S(1)}, bf16[1,128,2560]{2,1,0:T(8,128)(2,1)}, u32[]{:S(2)}) copy-start(bf16[1,128,2560]{2,1,0:T(8,128)(2,1)} %get-tuple-element.23.x_ref) | copy-start | bytes 1966084
  77.8 36.7 %copy-start.5 = (f32[128,40]{1,0:T(8,128)S(1)}, f32[128,40]{1,0:T(8,128)}, u32[]{:S(2)}) copy-start(f32[128,40]{1,0:T(8,128)} %get-tuple-element.38.enter_ref) | copy-start | bytes 61444
  77.8 36.7 %copy-start.9 = (bf16[128,64]{1,0:T(8,128)(2,1)S(1)}, bf16[128,64]{1,0:T(8,128)(2,1)}, u32[]{:S(2)}) copy-start(bf16[128,64]{1,0:T(8,128)(2,1)} %get-tuple-element.37.c_linked_ref) | copy-start | bytes 49156
  77.8 36.7 %copy-start.10 = (bf16[128,128]{1,0:T(8,128)(2,1)S(1)}, bf16[128,128]{1,0:T(8,128)(2,1)}, u32[]{:S(2)}) copy-start(bf16[128,128]{1,0:T(8,128)(2,1)} %get-tuple-element.36.scores_ref) | copy-start | bytes 98308
  77.8 36.7 %copy-start.13 = (f32[1,40]{1,0:T(1,128)S(1)}, f32[1,40]{1,0:T(1,128)}, u32[]{:S(2)}) copy-start(f32[1,40]{1,0:T(1,128)} %get-tuple-element.24.gain_ref) | copy-start | bytes 484
  110.7 5.6 %collective-permute-start.1 = (f32[160,8,128]{2,1,0:T(8,128)S(1)}, f32[160,8,128]{2,1,0:T(8,128)S(1)}, u32[]{:S(2)}, u32[]{:S(2)}) collective-permute-start(f32[160,8,128]{2,1,0:T(8,128)S(1)} %bitcast.9), channel_id=1, source_target_pairs={{0,16},{16,0},{1,17},{17,1},{2,18},{18,2},{3,19},{19,3},{4,20},{20... | collective-permute-start | bytes 1966088 | tf_op jit(solution)/shard_map/ppermute | solution.py:238

commit v2 on v1

v2 whole, which is shorter than its diff:
```python
import jax
import jax.numpy as jnp
from jax import lax
from jax.experimental import pallas as pl
from jax.experimental.pallas import tpu as pltpu
from jax.sharding import Mesh
from jax.sharding import PartitionSpec as P


SEQ = ("y", "x")
DP = ("z", "core")
F32 = jnp.float32
BF16 = jnp.bfloat16
CHUNK = 256
EXTRA = 128
OUT = 512


VMEM = pl.BlockSpec(memory_space=pltpu.VMEM)
HBM = pl.BlockSpec(memory_space=pltpu.HBM)
SMEM = pl.BlockSpec(memory_space=pltpu.SMEM)
ALL_VMEM = pltpu.CompilerParams(vmem_limit_bytes=67043328)
PARAMS = pltpu.CompilerParams(vmem_limit_bytes=48 * 1024 * 1024)


def dot(a, b, dims=((1,), (0,))):
    return lax.dot_general(a, b, (dims, ((), ())), preferred_element_type=F32)


def dot_nt(a, b):
    return dot(a, b, ((1,), (1,)))


def dot_tn(a, b):
    return dot(a, b, ((0,), (0,)))


def slot_index():
    return lax.axis_index("y") * lax.axis_size("x") + lax.axis_index("x")


def spread(values, first, count, width):
    rows = max(values.shape[0], 8)
    table = jnp.broadcast_to(values, (rows, 128))
    lane = lax.broadcasted_iota(jnp.int32, (rows, 128), 1) // width
    per = 128 // width
    parts = [
        jnp.take_along_axis(table, lane + (first + j), axis=1, mode="promise_in_bounds")
        for j in range(0, count, per)
    ]
    whole = jnp.concatenate(parts, axis=1) if len(parts) > 1 else parts[0]
    return whole[: values.shape[0]]


def count_started(starts, position):
    return sum((start <= position).astype(jnp.int32) for start in starts)


def states_kernel(
    lengths_hbm, order_hbm, layer_hbm, x_hbm, grad_hbm, step_hbm, bw_hbm, cw_hbm, rate_hbm,
    send_hbm, pushed_hbm, seen_hbm, mats_hbm, scores_hbm, enter_hbm,
    lengths_ref, order_ref, layer_ref, x_ref, grad_ref, step_ref, weights_ref, rate_ref,
    send_ref, pushed_ref, seen_ref, mats_ref, scores_ref, enter_ref, in_sems, out_sems,
):
    state = bw_hbm.shape[0]
    pairs = (
        (lengths_hbm, lengths_ref), (order_hbm, order_ref), (rate_hbm, rate_ref),
        (step_hbm, step_ref), (layer_hbm, layer_ref), (bw_hbm, weights_ref.at[:state]),
        (cw_hbm, weights_ref.at[state:]),
        (x_hbm, x_ref), (grad_hbm, grad_ref),
    )
    copies = [pltpu.make_async_copy(a, b, in_sems.at[i]) for i, (a, b) in enumerate(pairs)]
    for copy in copies:
        copy.start()
    leaving = []

    def leave_for(from_ref, to_ref):
        copy = pltpu.make_async_copy(from_ref, to_ref, out_sems.at[len(leaving)])
        copy.start()
        leaving.append(copy)

    rows, inner = x_ref.shape[1:]
    heads = rate_ref.shape[1]
    width = inner // heads
    docs = lengths_ref.shape[1]
    blocks = send_ref.shape[0]
    half = blocks // 2
    for copy in copies[:4]:
        copy.wait()
    first = order_ref[0, slot_index()] * rows
    starts = [jnp.int32(0)]
    for j in range(docs - 1):
        starts.append(starts[-1] + lengths_ref[0, j])
    across = (rows, rows)
    at_row = lax.broadcasted_iota(jnp.int32, across, 0)
    at_column = lax.broadcasted_iota(jnp.int32, across, 1)
    column = count_started(starts, first + at_row)
    row = count_started(starts, first + at_column)
    before = count_started(starts, first - 1)
    last = count_started(starts, first + rows - 1)
    tri = at_row >= at_column
    causal = tri & (column == row)
    linked = column[:, :state] == before
    in_last = column[:, :state] == last
    logs_up = -(step_ref[0] * rate_ref[...].T)
    spare = jnp.zeros((128 - heads, rows), F32)
    cum = lax.dot_general(
        tri.astype(F32), jnp.concatenate([logs_up, spare], axis=0), (((1,), (1,)), ((), ())),
        precision=lax.Precision.HIGHEST, preferred_element_type=F32,
    )
    steps = jnp.concatenate([step_ref[0], spare], axis=0).T
    enter = jnp.exp(cum)
    leave = steps * jnp.exp(-cum)
    enter_ref[...] = enter
    whole = enter[rows - 1 :, :]
    total = whole * (before == last).astype(F32)
    send_ref[:, :, inner:] = jnp.broadcast_to(total[None], (blocks, 8, 128))
    for copy in copies[4:7]:
        copy.wait()
    mats = dot_nt(layer_ref[0], weights_ref[...]).astype(BF16)
    b_mat = mats[:, :state]
    c_mat = mats[:, state:]
    scores_ref[0] = jnp.where(causal, dot_nt(c_mat, b_mat), 0.0).astype(BF16)
    scores_ref[1] = causal.astype(F32).astype(BF16)
    b_last = jnp.where(in_last, b_mat.astype(F32), 0.0).astype(BF16)
    c_linked = jnp.where(linked, c_mat.astype(F32), 0.0).astype(BF16)
    mats_ref[0] = b_mat
    mats_ref[1] = c_mat
    mats_ref[2] = c_linked
    mats_ref[3] = linked.astype(F32).astype(BF16)
    mats_ref[4] = in_last.astype(F32).astype(BF16)
    for copy in copies[7:]:
        copy.wait()
    per = CHUNK // width
    for at in range(0, inner, CHUNK):
        cols = slice(at, at + CHUNK)
        h = at // width
        pushed = (spread(leave, h, per, width) * x_ref[0, :, cols].astype(F32)).astype(BF16)
        seen = (spread(enter, h, per, width) * grad_ref[0, :, cols].astype(F32)).astype(BF16)
        pushed_ref[:, cols] = pushed
        seen_ref[:, cols] = seen
        own = dot_tn(b_last, pushed) * spread(whole, h, per, width)
        adj = dot_tn(c_linked, seen)
        send_ref[:half, :, cols] = own.reshape(half, 8, CHUNK)
        send_ref[half:, :, cols] = adj.reshape(half, 8, CHUNK)
        if (at + CHUNK) % OUT == 0:
            done = slice(at + CHUNK - OUT, at + CHUNK)
            leave_for(pushed_ref.at[:, done], pushed_hbm.at[:, done])
            leave_for(seen_ref.at[:, done], seen_hbm.at[:, done])
            end = at + CHUNK + (128 if at + CHUNK == inner else 0)
            done = slice(at + CHUNK - OUT, end)
            leave_for(send_ref.at[:, :, done], send_hbm.at[:, :, done])
        if at == 0:
            leave_for(mats_ref, mats_hbm)
            leave_for(scores_ref, scores_hbm)
            leave_for(enter_ref, enter_hbm)
    for copy in leaving:
        copy.wait()


def chain_kernel(order_ref, got_ref, out_ref, held_ref):
    blocks, _, inner = out_ref.shape
    heads = inner // 64
    for slot in range(blocks):
        held_ref[order_ref[0, slot]] = jnp.int32(slot)
    backward = slot_index() >= blocks // 2
    carry = jnp.zeros(out_ref.shape[1:], F32)
    for k in range(blocks):
        slot = held_ref[jnp.where(backward, blocks - 1 - k, k)]
        out_ref[slot] = carry
        if k < blocks - 1:
            totals = got_ref[slot, :, inner:]
            carry = carry * spread(totals, 0, heads, 64) + got_ref[slot, :, :inner]


def grads_kernel(
    layer_ref, got_ref, pushed_ref, seen_ref, mats_ref, scores_ref, enter_ref,
    came_ref, keep_ref, give_ref, ret_ref,
):
    rows, inner = pushed_ref.shape
    blocks = got_ref.shape[0]
    half = blocks // 2
    state = mats_ref.shape[2]
    whole = enter_ref[rows - 1 :, :]
    per = CHUNK // state
    for at in range(0, inner, CHUNK):
        cols = slice(at, at + CHUNK)
        back = got_ref[half:, :, cols].reshape(state, CHUNK)
        came_ref[:, cols] = got_ref[:half, :, cols].reshape(state, CHUNK).astype(BF16)
        ret_ref[:, cols] = (back * spread(whole, at // state, per, state)).astype(BF16)
    linked = mats_ref[3].astype(F32) > 0.5
    in_last = mats_ref[4].astype(F32) > 0.5
    pushed = pushed_ref[...]
    seen = seen_ref[...]
    causal = scores_ref[1].astype(F32) > 0.5
    mixing = jnp.where(causal, dot_nt(seen, pushed), 0.0).astype(BF16)
    d_b = dot_tn(mixing, mats_ref[1]) + jnp.where(in_last, dot_nt(pushed, ret_ref[...]), 0.0)
    d_c = dot(mixing, mats_ref[0]) + jnp.where(linked, dot_nt(seen, came_ref[...]), 0.0)
    scale = 1.0 / (rows * blocks * lax.axis_size("z") * lax.axis_size("core"))
    low = lax.axis_index("core") == 0
    mine = jnp.where(low, d_b, d_c).astype(BF16)
    other = jnp.where(low, d_c, d_b).astype(BF16)
    columns = layer_ref.shape[2] // 128
    for at in range(0, layer_ref.shape[2], CHUNK):
        tokens = layer_ref[0, :, at : at + CHUNK]
        for side, to_ref in ((other, give_ref), (mine, keep_ref)):
            part = dot_tn(side, tokens) * scale
            for r in range(state // 8):
                for c in range(CHUNK // 128):
                    tile = r * columns + at // 128 + c
                    to_ref[tile] = part[8 * r : 8 * r + 8, 128 * c : 128 * c + 128]


def output_kernel(x_ref, gain_ref, came_ref, pushed_ref, scores_ref, mats_ref, enter_ref, out_ref):
    inner = pushed_ref.shape[1]
    heads = gain_ref.shape[1]
    width = inner // heads
    scores = scores_ref[0]
    c_linked = mats_ref[2]
    enter = enter_ref[...]
    gain = jnp.concatenate([gain_ref[...].T, jnp.zeros((128 - heads, 1), F32)], axis=0).T
    per = CHUNK // width
    for at in range(0, inner, CHUNK):
        cols = slice(at, at + CHUNK)
        h = at // width
        mixed = dot(scores, pushed_ref[:, cols]) + dot(c_linked, came_ref[:, cols])
        skip = spread(gain, h, per, width) * x_ref[0, :, cols].astype(F32)
        out_ref[0, :, cols] = (spread(enter, h, per, width) * mixed + skip).astype(BF16)


def place(tiles_ref, whole_ref, b_hbm, c_hbm, to_b, sem):
    columns = whole_ref.shape[1] // 128
    for r in range(whole_ref.shape[0] // 8):
        for c in range(columns):
            whole_ref[8 * r : 8 * r + 8, 128 * c : 128 * c + 128] = tiles_ref[r * columns + c]

    @pl.when(to_b)
    def _():
        copy = pltpu.make_async_copy(whole_ref, b_hbm, sem)
        copy.start()
        copy.wait()

    @pl.when(jnp.logical_not(to_b))
    def _():
        copy = pltpu.make_async_copy(whole_ref, c_hbm, sem)
        copy.start()
        copy.wait()


def place_mine_kernel(tiles_ref, b_hbm, c_hbm, whole_ref, sem):
    place(tiles_ref, whole_ref, b_hbm, c_hbm, lax.axis_index("core") == 0, sem)


def place_other_kernel(tiles_ref, b_in, c_in, b_hbm, c_hbm, whole_ref, sem):
    place(tiles_ref, whole_ref, b_hbm, c_hbm, lax.axis_index("core") == 1, sem)


def shape(*dims, dtype=F32):
    return jax.ShapeDtypeStruct(dims, dtype)


def swap_cores(a):
    return lax.ppermute(a, "core", [(0, 1), (1, 0)])


def exchange(a, axes):
    return lax.all_to_all(a, axes, 0, 0, tiled=True)


def everywhere(a, axes):
    return exchange(jnp.broadcast_to(a[None], (lax.axis_size(axes),) + a.shape), axes)


def device_step(
    layer_in, scan_in, step_size, b_weight, c_weight, decay_rate, skip_gain, out_grad, doc_lengths,
    block_order,
):
    _, rows, inner = scan_in.shape
    width_in, state = b_weight.shape
    tile_cols = width_in // 128
    heads = decay_rate.shape[0]
    blocks = lax.axis_size(SEQ)
    docs = doc_lengths.shape[1]
    outs = (
        ((blocks, 8, inner + EXTRA), F32),
        ((rows, inner), BF16),
        ((rows, inner), BF16),
        ((5, rows, state), BF16),
        ((2, rows, rows), BF16),
        ((rows, 128), F32),
    )
    send, pushed, seen, mats, scores, enter = pl.pallas_call(
        states_kernel,
        out_shape=tuple(shape(*dims, dtype=dtype) for dims, dtype in outs),
        in_specs=[HBM] * 9,
        out_specs=(HBM,) * 6,
        scratch_shapes=[
            pltpu.SMEM((1, docs), jnp.int32),
            pltpu.SMEM((1, blocks), jnp.int32),
            pltpu.VMEM((1, rows, width_in), BF16),
            pltpu.VMEM((1, rows, inner), BF16),
            pltpu.VMEM((1, rows, inner), BF16),
            pltpu.VMEM((1, heads, rows), F32),
            pltpu.VMEM((2 * state, width_in), BF16),
            pltpu.VMEM((1, heads), F32),
            *[pltpu.VMEM(dims, dtype) for dims, dtype in outs],
            pltpu.SemaphoreType.DMA((9,)),
            pltpu.SemaphoreType.DMA((3 * (inner // OUT) + 3,)),
        ],
        compiler_params=ALL_VMEM,
    )(
        doc_lengths, block_order, layer_in, scan_in, out_grad, jnp.swapaxes(step_size, 1, 2),
        b_weight.T, c_weight.T, decay_rate[None],
    )
    cost = pl.CostEstimate(flops=10**9, bytes_accessed=10**6, transcendentals=0)
    got = exchange(send, SEQ)
    carried = pl.pallas_call(
        chain_kernel,
        out_shape=shape(blocks, 8, inner),
        in_specs=[SMEM, VMEM],
        out_specs=VMEM,
        scratch_shapes=[pltpu.SMEM((blocks,), jnp.int32)],
        compiler_params=PARAMS,
    )(block_order, got)
    back = exchange(carried, SEQ)
    came, keep, give = pl.pallas_call(
        grads_kernel,
        out_shape=(
            shape(state, inner, dtype=BF16),
            shape(state // 8 * tile_cols, 8, 128),
            shape(state // 8 * tile_cols, 8, 128),
        ),
        in_specs=[VMEM] * 7,
        out_specs=(VMEM,) * 3,
        scratch_shapes=[pltpu.VMEM((state, inner), BF16)],
        compiler_params=PARAMS,
        cost_estimate=cost,
    )(layer_in, back, pushed, seen, mats, scores, enter)
    given = swap_cores(give)
    scan_out = pl.pallas_call(
        output_kernel,
        out_shape=shape(1, rows, inner, dtype=BF16),
        in_specs=[VMEM] * 7,
        out_specs=VMEM,
        compiler_params=PARAMS,
        cost_estimate=cost,
    )(scan_in, skip_gain[None], came, pushed, scores, mats, enter)
    local = keep + given
    tiles = local.shape[0] // blocks
    share = jnp.sum(exchange(local.reshape(blocks, tiles, 8, 128), SEQ), axis=0)
    share = jnp.sum(everywhere(share, "z"), axis=0)
    mine = everywhere(share, SEQ).reshape(local.shape)
    other = swap_cores(mine)
    halves = (shape(state, width_in), shape(state, width_in))
    scratch = [pltpu.VMEM((state, width_in), F32), pltpu.SemaphoreType.DMA]
    partly = pl.pallas_call(
        place_mine_kernel,
        out_shape=halves,
        in_specs=[VMEM],
        out_specs=(HBM, HBM),
        scratch_shapes=scratch,
        compiler_params=PARAMS,
        cost_estimate=cost,
    )(mine)
    b_grad, c_grad = pl.pallas_call(
        place_other_kernel,
        out_shape=halves,
        in_specs=[VMEM, HBM, HBM],
        out_specs=(HBM, HBM),
        scratch_shapes=scratch,
        input_output_aliases={1: 0, 2: 1},
        compiler_params=PARAMS,
    )(other, *partly)
    return scan_out, b_grad.T, c_grad.T


def solution(mesh):
    seq = mesh.shape["seq"]
    side = 4 if seq % 4 == 0 else 1
    split = Mesh(
        mesh.devices.reshape(mesh.shape["dp"] // 2, 2, seq // side, side), ("z", "core", "y", "x")
    )
    rows = P(DP, SEQ, None)
    group = P(DP, None)
    in_specs = (rows, rows, rows, P(), P(), P(), P(), rows, group, group)
    return jax.shard_map(
        device_step, mesh=split, in_specs=in_specs, out_specs=(rows, P(), P()), check_vma=False
    )
```

time: 118 us -> 117 us (level)
    pallas_call x5 -> x6, Pallas kernels: 11.2 us -> 10.2 us  [the longest x1 4.14 us: device_step(): pl.pallas_call(states_kernel, out_shape=tuple((shape(*dims, dtype=dtype)...]
  transfers between devices with their start and end apart: 2 -> 2, of which waited for: 1 -> 1; matrix products, arithmetic and copies ran while one was open for 0% -> 0% of each run, Pallas kernels for 1% -> 2%
where the time goes in v2:
time: 117 us; the launch traced here: 116 us
  blocking collectives  96.9 us (83%)
  Pallas kernels  10.2 us (9%)
  starting transfers between devices  6.46 us (6%)
  waiting for transfers between devices  1.73 us (1%)
    all_to_all x5, blocking collectives, exchange(): return lax.all_to_all(a, axes, 0, 0, tiled=True)  96.9 us
    ppermute x2, starting transfers between devices, swap_cores(): return lax.ppermute(a, 'core', [(0, 1), (1, 0)])  6.46 us
    pallas_call x1, Pallas kernels, device_step(): pl.pallas_call(states_kernel, out_shape=tuple((shape(*dims, dtype=dtype)...  4.14 us
  transfers between devices with their start and end apart: 2, of which 1 were waited for; matrix products, arithmetic and copies ran while one was open for 0% of the time, Pallas kernels for 2%

profile of v2, /device:TPU:1, one launch (start us, length us, event | category | flops | bytes accessed | tf_op | source)
XLA Modules:
  0.0 116.4 jit_solution(14164162177038664435)
XLA Ops:
  0.6 4.1 %shard_map.121 = (f32[16,8,2688]{2,1,0:T(8,128)}, bf16[128,2560]{1,0:T(8,128)(2,1)}, bf16[128,2560]{1,0:T(8,128)(2,1)}, bf16[5,128,64]{2,1,0:T(8,128)(2,1)}, bf1...) custom-call(s32[1,4]{1,0:T(1,128)} %lengths_hbm.1, s32[1,16]{1,0:T(1,128)} %order_ref.1, bf16[1,128,2560]{2,1,0:T(8,128)(2,1)} %layer_ref.1, ...), custom_call_target="tpu_custom_call" | custom-call | tf_op jit(solution)/shard_map/pallas_call | solution.py:292
  4.8 0.0 copy-start.2
  4.8 27.4 %all_to_all.25.got_ref = f32[16,8,2688]{2,1,0:T(8,128)S(1)} all-to-all(f32[16,8,2688]{2,1,0:T(8,128)} %get-tuple-element.16), channel_id=1, replica_groups=mesh['z'=8,'core'=2,'y'=4,'x'=4] {'y','x'}, dimensions={0} | all-to-all | bytes 2752512 | tf_op jit(solution)/shard_map/all_to_all | solution.py:267
  32.2 0.0 copy-done.2
  32.2 1.5 %shard_map.122 = f32[16,8,2560]{2,1,0:T(8,128)S(1)} custom-call(s32[1,16]{1,0:T(1,128)S(1)} %copy-done.2, f32[16,8,2688]{2,1,0:T(8,128)S(1)} %all_to_all.25.got_ref), custom_call_target="tpu_custom_call" | custom-call | tf_op jit(solution)/shard_map/pallas_call | solution.py:317
  33.7 0.0 copy-start
  33.7 0.0 copy-start.3
  33.7 0.0 copy-start.4
  33.7 0.0 copy-start.5
  33.8 0.0 copy-start.6
  33.8 0.0 copy-start.7
  33.8 21.6 %all_to_all.26.got_ref = f32[16,8,2560]{2,1,0:T(8,128)S(1)} all-to-all(f32[16,8,2560]{2,1,0:T(8,128)S(1)} %shard_map.122), channel_id=1, replica_groups=mesh['z'=8,'core'=2,'y'=4,'x'=4] {'y','x'}, dimensions={0} | all-to-all | bytes 2621440 | tf_op jit(solution)/shard_map/all_to_all | solution.py:267
  55.4 0.0 copy-done
  55.4 0.0 copy-done.3
  55.4 0.0 copy-done.4
  55.4 0.0 copy-done.5
  55.4 0.0 copy-done.6
  55.4 0.0 copy-done.7
  55.4 1.3 %shard_map.123 = (bf16[64,2560]{1,0:T(8,128)(2,1)S(1)}, f32[160,8,128]{2,1,0:T(8,128)S(1)}, f32[160,8,128]{2,1,0:T(8,128)S(1)}) custom-call(bf16[1,128,2560]{2,1,0:T(8,128)(2,1)S(1)} %copy-done, f32[16,8,2560]{2,1,0:T(8,128)S(1)} %all_to_all.26.got_ref, bf16[128,2560]{1,0:T(8,128)(2,1)S(1)} %copy-done.3, bf16[128,2560]{1,0:T(8,128)(2,1)S(1)} %copy-done.4, ...), custom_call_target="tpu_custom_call" | custom-call | flops 1000000000 | bytes 1000000 | tf_op jit(solution)/shard_map/pallas_call | solution.py:326
  56.7 2.6 %collective-permute-start = (f32[160,8,128]{2,1,0:T(8,128)S(1)}, f32[160,8,128]{2,1,0:T(8,128)S(1)}, u32[]{:S(2)}, u32[]{:S(2)}) collective-permute-start(f32[160,8,128]{2,1,0:T(8,128)S(1)} %get-tuple-element.24), channel_id=1, source_target_pairs={{0,16},{16,0},{1,17},{17,1},{2,18},{18,2},{3,19},{19,3},{4,20},{20... | collective-permute-start | bytes 1966088 | tf_op jit(solution)/shard_map/ppermute | solution.py:263
  59.4 1.7 %collective-permute-done = f32[160,8,128]{2,1,0:T(8,128)S(1)} collective-permute-done((f32[160,8,128]{2,1,0:T(8,128)S(1)}, f32[160,8,128]{2,1,0:T(8,128)S(1)}, u32[]{:S(2)}, u32[]{:S(2)}) %collective-permute-start) | collective-permute-done | bytes 655392 | tf_op jit(solution)/shard_map/ppermute | solution.py:263
  61.1 0.1 add.3
  61.2 15.1 %all_to_all.27 = f32[16,10,8,128]{3,2,1,0:T(8,128)S(1)} all-to-all(f32[16,10,8,128]{3,2,1,0:T(8,128)S(1)} %bitcast.12), channel_id=1, replica_groups=mesh['z'=8,'core'=2,'y'=4,'x'=4] {'y','x'}, dimensions={0} | all-to-all | bytes 1310720 | tf_op jit(solution)/shard_map/all_to_all | solution.py:267
  76.4 0.0 copy-start.1
  76.4 0.0 copy-start.8
  76.4 18.9 %all_to_all.28 = f32[8,10,8,128]{3,2,1,0:T(8,128)S(1)} all-to-all(f32[8,10,8,128]{3,2,1,0:T(8,128)S(1)} %broadcast_in_dim.20), channel_id=1, replica_groups=mesh['z'=8,'core'=2,'y'=4,'x'=4] {'z'}, dimensions={0} | all-to-all | bytes 655360 | tf_op jit(solution)/shard_map/all_to_all | solution.py:267
  95.4 13.9 %all_to_all.29 = f32[16,10,8,128]{3,2,1,0:T(8,128)S(1)} all-to-all(f32[16,10,8,128]{3,2,1,0:T(8,128)S(1)} %broadcast_in_dim.21), channel_id=1, replica_groups=mesh['z'=8,'core'=2,'y'=4,'x'=4] {'y','x'}, dimensions={0} | all-to-all | bytes 1310720 | tf_op jit(solution)/shard_map/all_to_all | solution.py:267
  109.2 3.8 %collective-permute-start.1 = (f32[160,8,128]{2,1,0:T(8,128)S(1)}, f32[160,8,128]{2,1,0:T(8,128)S(1)}, u32[]{:S(2)}, u32[]{:S(2)}) collective-permute-start(f32[160,8,128]{2,1,0:T(8,128)S(1)} %bitcast.9), channel_id=1, source_target_pairs={{0,16},{16,0},{1,17},{17,1},{2,18},{18,2},{3,19},{19,3},{4,20},{20... | collective-permute-start | bytes 1966088 | tf_op jit(solution)/shard_map/ppermute | solution.py:263
  113.1 0.0 copy-done.1
  113.1 0.0 copy-done.8
  113.1 1.5 %shard_map.124 = bf16[1,128,2560]{2,1,0:T(8,128)(2,1)} custom-call(bf16[1,128,2560]{2,1,0:T(8,128)(2,1)S(1)} %copy-done.1, f32[1,40]{1,0:T(1,128)S(1)} %bitcast.11, bf16[64,2560]{1,0:T(8,128)(2,1)S(1)} %get-tuple-element.22.came_ref, bf16[128,2560]{1,0:T(8,128)(2,1)S(1)} %copy-done.3, bf16[2,128,128]{2,1,0:T(8,128)(2,1)S(1)} %copy-done.6, ...), custom_call_target="tpu_custom_call" | custom-call | flops 1000000000 | bytes 1000000 | tf_op jit(solution)/shard_map/pallas_call | solution.py:340
  114.6 0.9 shard_map.125
  115.5 0.0 collective-permute-done.1.tiles_ref
  115.5 0.9 shard_map.126
  (4 shorter events, 0.1 us)
Async XLA Ops:
  4.8 27.4 %copy-start.2 = (s32[1,16]{1,0:T(1,128)S(1)}, s32[1,16]{1,0:T(1,128)}, u32[]{:S(2)}) copy-start(s32[1,16]{1,0:T(1,128)} %order_ref.1) | copy-start | bytes 196
  33.7 21.7 %copy-start = (bf16[1,128,2560]{2,1,0:T(8,128)(2,1)S(1)}, bf16[1,128,2560]{2,1,0:T(8,128)(2,1)}, u32[]{:S(2)}) copy-start(bf16[1,128,2560]{2,1,0:T(8,128)(2,1)} %layer_ref.1) | copy-start | bytes 1966084
  33.7 21.6 %copy-start.3 = (bf16[128,2560]{1,0:T(8,128)(2,1)S(1)}, bf16[128,2560]{1,0:T(8,128)(2,1)}, u32[]{:S(2)}) copy-start(bf16[128,2560]{1,0:T(8,128)(2,1)} %get-tuple-element.17.pushed_ref) | copy-start | bytes 1966084
  33.7 21.6 %copy-start.4 = (bf16[128,2560]{1,0:T(8,128)(2,1)S(1)}, bf16[128,2560]{1,0:T(8,128)(2,1)}, u32[]{:S(2)}) copy-start(bf16[128,2560]{1,0:T(8,128)(2,1)} %get-tuple-element.18.seen_ref) | copy-start | bytes 1966084
  33.7 21.6 %copy-start.5 = (bf16[5,128,64]{2,1,0:T(8,128)(2,1)S(1)}, bf16[5,128,64]{2,1,0:T(8,128)(2,1)}, u32[]{:S(2)}) copy-start(bf16[5,128,64]{2,1,0:T(8,128)(2,1)} %get-tuple-element.19.mats_ref) | copy-start | bytes 245764
  33.8 21.6 %copy-start.6 = (bf16[2,128,128]{2,1,0:T(8,128)(2,1)S(1)}, bf16[2,128,128]{2,1,0:T(8,128)(2,1)}, u32[]{:S(2)}) copy-start(bf16[2,128,128]{2,1,0:T(8,128)(2,1)} %get-tuple-element.20.scores_ref) | copy-start | bytes 196612
  33.8 21.6 %copy-start.7 = (f32[128,128]{1,0:T(8,128)S(1)}, f32[128,128]{1,0:T(8,128)}, u32[]{:S(2)}) copy-start(f32[128,128]{1,0:T(8,128)} %get-tuple-element.21.enter_ref) | copy-start | bytes 196612
  56.7 4.4 %collective-permute-start = (f32[160,8,128]{2,1,0:T(8,128)S(1)}, f32[160,8,128]{2,1,0:T(8,128)S(1)}, u32[]{:S(2)}, u32[]{:S(2)}) collective-permute-start(f32[160,8,128]{2,1,0:T(8,128)S(1)} %get-tuple-element.24), channel_id=1, source_target_pairs={{0,16},{16,0},{1,17},{17,1},{2,18},{18,2},{3,19},{19,3},{4,20},{20... | collective-permute-start | bytes 1966088 | tf_op jit(solution)/shard_map/ppermute | solution.py:263
  76.4 36.7 %copy-start.1 = (bf16[1,128,2560]{2,1,0:T(8,128)(2,1)S(1)}, bf16[1,128,2560]{2,1,0:T(8,128)(2,1)}, u32[]{:S(2)}) copy-start(bf16[1,128,2560]{2,1,0:T(8,128)(2,1)} %x_ref.1) | copy-start | bytes 1966084
  76.4 36.7 %copy-start.8 = (f32[40]{0:T(128)S(1)}, f32[40]{0:T(128)}, u32[]{:S(2)}) copy-start(f32[40]{0:T(128)} %param.16) | copy-start | bytes 484
  109.2 6.2 %collective-permute-start.1 = (f32[160,8,128]{2,1,0:T(8,128)S(1)}, f32[160,8,128]{2,1,0:T(8,128)S(1)}, u32[]{:S(2)}, u32[]{:S(2)}) collective-permute-start(f32[160,8,128]{2,1,0:T(8,128)S(1)} %bitcast.9), channel_id=1, source_target_pairs={{0,16},{16,0},{1,17},{17,1},{2,18},{18,2},{3,19},{19,3},{4,20},{20... | collective-permute-start | bytes 1966088 | tf_op jit(solution)/shard_map/ppermute | solution.py:263

commit v3 on v2

--- a/solution.py
+++ b/solution.py
@@ -158,19 +158,21 @@
         copy.wait()
 
 
-def chain_kernel(order_ref, got_ref, out_ref, held_ref):
+def chain_kernel(order_ref, got_ref, out_ref, held_ref, totals_ref):
     blocks, _, inner = out_ref.shape
     heads = inner // 64
     for slot in range(blocks):
         held_ref[order_ref[0, slot]] = jnp.int32(slot)
     backward = slot_index() >= blocks // 2
+    totals = spread(got_ref[:, 0, inner:], 0, heads, 64)
+    for slot in range(blocks):
+        totals_ref[slot] = jnp.broadcast_to(totals[slot : slot + 1], (1, inner))
     carry = jnp.zeros(out_ref.shape[1:], F32)
     for k in range(blocks):
         slot = held_ref[jnp.where(backward, blocks - 1 - k, k)]
         out_ref[slot] = carry
         if k < blocks - 1:
-            totals = got_ref[slot, :, inner:]
-            carry = carry * spread(totals, 0, heads, 64) + got_ref[slot, :, :inner]
+            carry = carry * totals_ref[slot] + got_ref[slot, :, :inner]
 
 
 def grads_kernel(
@@ -319,7 +321,7 @@
         out_shape=shape(blocks, 8, inner),
         in_specs=[SMEM, VMEM],
         out_specs=VMEM,
-        scratch_shapes=[pltpu.SMEM((blocks,), jnp.int32)],
+        scratch_shapes=[pltpu.SMEM((blocks,), jnp.int32), pltpu.VMEM((blocks, 1, inner), F32)],
         compiler_params=PARAMS,
     )(block_order, got)
     back = exchange(carried, SEQ)

time: 117 us -> 116 us (level)
  no operation moved by 1% of the time
where the time goes in v3:
time: 116 us
  blocking collectives  96.9 us (84%)
  Pallas kernels  9.6 us (8%)
  starting transfers between devices  6.46 us (6%)
  waiting for transfers between devices  1.73 us (1%)
    all_to_all x5, blocking collectives, exchange(): return lax.all_to_all(a, axes, 0, 0, tiled=True)  96.9 us
    ppermute x2, starting transfers between devices, swap_cores(): return lax.ppermute(a, 'core', [(0, 1), (1, 0)])  6.46 us
    pallas_call x1, Pallas kernels, device_step(): pl.pallas_call(states_kernel, out_shape=tuple((shape(*dims, dtype=dtype)...  4.14 us
  transfers between devices with their start and end apart: 2, of which 1 were waited for; matrix products, arithmetic and copies ran while one was open for 0% of the time, Pallas kernels for 2%

profile of v3, /device:TPU:1, one launch (start us, length us, event | category | flops | bytes accessed | tf_op | source)
XLA Modules:
  0.0 115.8 jit_solution(15993755176550789054)
XLA Ops:
  0.6 4.1 %shard_map.121 = (f32[16,8,2688]{2,1,0:T(8,128)}, bf16[128,2560]{1,0:T(8,128)(2,1)}, bf16[128,2560]{1,0:T(8,128)(2,1)}, bf16[5,128,64]{2,1,0:T(8,128)(2,1)}, bf1...) custom-call(s32[1,4]{1,0:T(1,128)} %lengths_hbm.1, s32[1,16]{1,0:T(1,128)} %order_ref.1, bf16[1,128,2560]{2,1,0:T(8,128)(2,1)} %layer_ref.1, ...), custom_call_target="tpu_custom_call" | custom-call | tf_op jit(solution)/shard_map/pallas_call | solution.py:294
  4.8 0.0 copy-start.2
  4.8 27.4 %all_to_all.25.got_ref = f32[16,8,2688]{2,1,0:T(8,128)S(1)} all-to-all(f32[16,8,2688]{2,1,0:T(8,128)} %get-tuple-element.16), channel_id=1, replica_groups=mesh['z'=8,'core'=2,'y'=4,'x'=4] {'y','x'}, dimensions={0} | all-to-all | bytes 2752512 | tf_op jit(solution)/shard_map/all_to_all | solution.py:269
  32.2 0.0 copy-done.2
  32.2 0.8 shard_map.122
  33.1 0.0 copy-start
  33.1 0.0 copy-start.3
  33.1 0.0 copy-start.4
  33.1 0.0 copy-start.5
  33.1 0.0 copy-start.6
  33.1 0.0 copy-start.7
  33.2 21.6 %all_to_all.26.got_ref = f32[16,8,2560]{2,1,0:T(8,128)S(1)} all-to-all(f32[16,8,2560]{2,1,0:T(8,128)S(1)} %shard_map.122), channel_id=1, replica_groups=mesh['z'=8,'core'=2,'y'=4,'x'=4] {'y','x'}, dimensions={0} | all-to-all | bytes 2621440 | tf_op jit(solution)/shard_map/all_to_all | solution.py:269
  54.7 0.0 copy-done
  54.7 0.0 copy-done.3
  54.7 0.0 copy-done.4
  54.7 0.0 copy-done.5
  54.8 0.0 copy-done.6
  54.8 0.0 copy-done.7
  54.8 1.3 %shard_map.123 = (bf16[64,2560]{1,0:T(8,128)(2,1)S(1)}, f32[160,8,128]{2,1,0:T(8,128)S(1)}, f32[160,8,128]{2,1,0:T(8,128)S(1)}) custom-call(bf16[1,128,2560]{2,1,0:T(8,128)(2,1)S(1)} %copy-done, f32[16,8,2560]{2,1,0:T(8,128)S(1)} %all_to_all.26.got_ref, bf16[128,2560]{1,0:T(8,128)(2,1)S(1)} %copy-done.3, bf16[128,2560]{1,0:T(8,128)(2,1)S(1)} %copy-done.4, ...), custom_call_target="tpu_custom_call" | custom-call | flops 1000000000 | bytes 1000000 | tf_op jit(solution)/shard_map/pallas_call | solution.py:328
  56.1 2.6 %collective-permute-start = (f32[160,8,128]{2,1,0:T(8,128)S(1)}, f32[160,8,128]{2,1,0:T(8,128)S(1)}, u32[]{:S(2)}, u32[]{:S(2)}) collective-permute-start(f32[160,8,128]{2,1,0:T(8,128)S(1)} %get-tuple-element.24), channel_id=1, source_target_pairs={{0,16},{16,0},{1,17},{17,1},{2,18},{18,2},{3,19},{19,3},{4,20},{20... | collective-permute-start | bytes 1966088 | tf_op jit(solution)/shard_map/ppermute | solution.py:265
  58.7 1.7 %collective-permute-done = f32[160,8,128]{2,1,0:T(8,128)S(1)} collective-permute-done((f32[160,8,128]{2,1,0:T(8,128)S(1)}, f32[160,8,128]{2,1,0:T(8,128)S(1)}, u32[]{:S(2)}, u32[]{:S(2)}) %collective-permute-start) | collective-permute-done | bytes 655392 | tf_op jit(solution)/shard_map/ppermute | solution.py:265
  60.5 0.1 add.3
  60.5 15.1 %all_to_all.27 = f32[16,10,8,128]{3,2,1,0:T(8,128)S(1)} all-to-all(f32[16,10,8,128]{3,2,1,0:T(8,128)S(1)} %bitcast.12), channel_id=1, replica_groups=mesh['z'=8,'core'=2,'y'=4,'x'=4] {'y','x'}, dimensions={0} | all-to-all | bytes 1310720 | tf_op jit(solution)/shard_map/all_to_all | solution.py:269
  75.7 0.0 copy-start.1
  75.8 0.0 copy-start.8
  75.8 18.9 %all_to_all.28 = f32[8,10,8,128]{3,2,1,0:T(8,128)S(1)} all-to-all(f32[8,10,8,128]{3,2,1,0:T(8,128)S(1)} %broadcast_in_dim.20), channel_id=1, replica_groups=mesh['z'=8,'core'=2,'y'=4,'x'=4] {'z'}, dimensions={0} | all-to-all | bytes 655360 | tf_op jit(solution)/shard_map/all_to_all | solution.py:269
  94.7 13.9 %all_to_all.29 = f32[16,10,8,128]{3,2,1,0:T(8,128)S(1)} all-to-all(f32[16,10,8,128]{3,2,1,0:T(8,128)S(1)} %broadcast_in_dim.21), channel_id=1, replica_groups=mesh['z'=8,'core'=2,'y'=4,'x'=4] {'y','x'}, dimensions={0} | all-to-all | bytes 1310720 | tf_op jit(solution)/shard_map/all_to_all | solution.py:269
  108.6 3.8 %collective-permute-start.1 = (f32[160,8,128]{2,1,0:T(8,128)S(1)}, f32[160,8,128]{2,1,0:T(8,128)S(1)}, u32[]{:S(2)}, u32[]{:S(2)}) collective-permute-start(f32[160,8,128]{2,1,0:T(8,128)S(1)} %bitcast.9), channel_id=1, source_target_pairs={{0,16},{16,0},{1,17},{17,1},{2,18},{18,2},{3,19},{19,3},{4,20},{20... | collective-permute-start | bytes 1966088 | tf_op jit(solution)/shard_map/ppermute | solution.py:265
  112.4 0.0 copy-done.1
  112.4 0.0 copy-done.8
  112.4 1.5 %shard_map.124 = bf16[1,128,2560]{2,1,0:T(8,128)(2,1)} custom-call(bf16[1,128,2560]{2,1,0:T(8,128)(2,1)S(1)} %copy-done.1, f32[1,40]{1,0:T(1,128)S(1)} %bitcast.11, bf16[64,2560]{1,0:T(8,128)(2,1)S(1)} %get-tuple-element.22.came_ref, bf16[128,2560]{1,0:T(8,128)(2,1)S(1)} %copy-done.3, bf16[2,128,128]{2,1,0:T(8,128)(2,1)S(1)} %copy-done.6, ...), custom_call_target="tpu_custom_call" | custom-call | flops 1000000000 | bytes 1000000 | tf_op jit(solution)/shard_map/pallas_call | solution.py:342
  114.0 0.9 shard_map.125
  114.8 0.0 collective-permute-done.1.tiles_ref
  114.9 0.9 shard_map.126
  (4 shorter events, 0.1 us)
Async XLA Ops:
  4.8 27.4 %copy-start.2 = (s32[1,16]{1,0:T(1,128)S(1)}, s32[1,16]{1,0:T(1,128)}, u32[]{:S(2)}) copy-start(s32[1,16]{1,0:T(1,128)} %order_ref.1) | copy-start | bytes 196
  33.1 21.7 %copy-start = (bf16[1,128,2560]{2,1,0:T(8,128)(2,1)S(1)}, bf16[1,128,2560]{2,1,0:T(8,128)(2,1)}, u32[]{:S(2)}) copy-start(bf16[1,128,2560]{2,1,0:T(8,128)(2,1)} %layer_ref.1) | copy-start | bytes 1966084
  33.1 21.6 %copy-start.3 = (bf16[128,2560]{1,0:T(8,128)(2,1)S(1)}, bf16[128,2560]{1,0:T(8,128)(2,1)}, u32[]{:S(2)}) copy-start(bf16[128,2560]{1,0:T(8,128)(2,1)} %get-tuple-element.17.pushed_ref) | copy-start | bytes 1966084
  33.1 21.6 %copy-start.4 = (bf16[128,2560]{1,0:T(8,128)(2,1)S(1)}, bf16[128,2560]{1,0:T(8,128)(2,1)}, u32[]{:S(2)}) copy-start(bf16[128,2560]{1,0:T(8,128)(2,1)} %get-tuple-element.18.seen_ref) | copy-start | bytes 1966084
  33.1 21.6 %copy-start.5 = (bf16[5,128,64]{2,1,0:T(8,128)(2,1)S(1)}, bf16[5,128,64]{2,1,0:T(8,128)(2,1)}, u32[]{:S(2)}) copy-start(bf16[5,128,64]{2,1,0:T(8,128)(2,1)} %get-tuple-element.19.mats_ref) | copy-start | bytes 245764
  33.1 21.6 %copy-start.6 = (bf16[2,128,128]{2,1,0:T(8,128)(2,1)S(1)}, bf16[2,128,128]{2,1,0:T(8,128)(2,1)}, u32[]{:S(2)}) copy-start(bf16[2,128,128]{2,1,0:T(8,128)(2,1)} %get-tuple-element.20.scores_ref) | copy-start | bytes 196612
  33.1 21.6 %copy-start.7 = (f32[128,128]{1,0:T(8,128)S(1)}, f32[128,128]{1,0:T(8,128)}, u32[]{:S(2)}) copy-start(f32[128,128]{1,0:T(8,128)} %get-tuple-element.21.enter_ref) | copy-start | bytes 196612
  56.1 4.4 %collective-permute-start = (f32[160,8,128]{2,1,0:T(8,128)S(1)}, f32[160,8,128]{2,1,0:T(8,128)S(1)}, u32[]{:S(2)}, u32[]{:S(2)}) collective-permute-start(f32[160,8,128]{2,1,0:T(8,128)S(1)} %get-tuple-element.24), channel_id=1, source_target_pairs={{0,16},{16,0},{1,17},{17,1},{2,18},{18,2},{3,19},{19,3},{4,20},{20... | collective-permute-start | bytes 1966088 | tf_op jit(solution)/shard_map/ppermute | solution.py:265
  75.7 36.7 %copy-start.1 = (bf16[1,128,2560]{2,1,0:T(8,128)(2,1)S(1)}, bf16[1,128,2560]{2,1,0:T(8,128)(2,1)}, u32[]{:S(2)}) copy-start(bf16[1,128,2560]{2,1,0:T(8,128)(2,1)} %x_ref.1) | copy-start | bytes 1966084
  75.8 36.7 %copy-start.8 = (f32[40]{0:T(128)S(1)}, f32[40]{0:T(128)}, u32[]{:S(2)}) copy-start(f32[40]{0:T(128)} %param.16) | copy-start | bytes 484
  108.6 6.2 %collective-permute-start.1 = (f32[160,8,128]{2,1,0:T(8,128)S(1)}, f32[160,8,128]{2,1,0:T(8,128)S(1)}, u32[]{:S(2)}, u32[]{:S(2)}) collective-permute-start(f32[160,8,128]{2,1,0:T(8,128)S(1)} %bitcast.9), channel_id=1, source_target_pairs={{0,16},{16,0},{1,17},{17,1},{2,18},{18,2},{3,19},{19,3},{4,20},{20... | collective-permute-start | bytes 1966088 | tf_op jit(solution)/shard_map/ppermute | solution.py:265

commit v4 on v3

--- a/solution.py
+++ b/solution.py
@@ -1,3 +1,5 @@
+import functools
+
 import jax
 import jax.numpy as jnp
 from jax import lax
@@ -177,7 +179,7 @@
 
 def grads_kernel(
     layer_ref, got_ref, pushed_ref, seen_ref, mats_ref, scores_ref, enter_ref,
-    came_ref, keep_ref, give_ref, ret_ref,
+    came_ref, mine_ref, give_ref, ret_ref,
 ):
     rows, inner = pushed_ref.shape
     blocks = got_ref.shape[0]
@@ -200,17 +202,22 @@
     d_c = dot(mixing, mats_ref[0]) + jnp.where(linked, dot_nt(seen, came_ref[...]), 0.0)
     scale = 1.0 / (rows * blocks * lax.axis_size("z") * lax.axis_size("core"))
     low = lax.axis_index("core") == 0
-    mine = jnp.where(low, d_b, d_c).astype(BF16)
-    other = jnp.where(low, d_c, d_b).astype(BF16)
+    mine_ref[...] = jnp.where(low, d_b, d_c).astype(BF16)
+    weight_tiles(jnp.where(low, d_c, d_b).astype(BF16), layer_ref, scale, give_ref)
+
+
+def weight_tiles(side, layer_ref, scale, to_ref):
     columns = layer_ref.shape[2] // 128
     for at in range(0, layer_ref.shape[2], CHUNK):
-        tokens = layer_ref[0, :, at : at + CHUNK]
-        for side, to_ref in ((other, give_ref), (mine, keep_ref)):
-            part = dot_tn(side, tokens) * scale
-            for r in range(state // 8):
-                for c in range(CHUNK // 128):
-                    tile = r * columns + at // 128 + c
-                    to_ref[tile] = part[8 * r : 8 * r + 8, 128 * c : 128 * c + 128]
+        part = dot_tn(side, layer_ref[0, :, at : at + CHUNK]) * scale
+        for r in range(side.shape[1] // 8):
+            for c in range(CHUNK // 128):
+                tile = r * columns + at // 128 + c
+                to_ref[tile] = part[8 * r : 8 * r + 8, 128 * c : 128 * c + 128]
+
+
+def keep_kernel(scale, layer_ref, mine_ref, keep_ref):
+    weight_tiles(mine_ref[...], layer_ref, scale, keep_ref)
 
 
 def output_kernel(x_ref, gain_ref, came_ref, pushed_ref, scores_ref, mats_ref, enter_ref, out_ref):
@@ -230,31 +237,25 @@
         out_ref[0, :, cols] = (spread(enter, h, per, width) * mixed + skip).astype(BF16)
 
 
-def place(tiles_ref, whole_ref, b_hbm, c_hbm, to_b, sem):
-    columns = whole_ref.shape[1] // 128
-    for r in range(whole_ref.shape[0] // 8):
-        for c in range(columns):
-            whole_ref[8 * r : 8 * r + 8, 128 * c : 128 * c + 128] = tiles_ref[r * columns + c]
-
-    @pl.when(to_b)
+def unpack_kernel(mine_ref, other_ref, b_ref, c_ref):
+    columns = b_ref.shape[1] // 128
+
+    def write(from_ref, to_ref):
+        for r in range(to_ref.shape[0] // 8):
+            for c in range(columns):
+                to_ref[8 * r : 8 * r + 8, 128 * c : 128 * c + 128] = from_ref[r * columns + c]
+
+    first = lax.axis_index("core") == 0
+
+    @pl.when(first)
     def _():
-        copy = pltpu.make_async_copy(whole_ref, b_hbm, sem)
-        copy.start()
-        copy.wait()
-
-    @pl.when(jnp.logical_not(to_b))
+        write(mine_ref, b_ref)
+        write(other_ref, c_ref)
+
+    @pl.when(jnp.logical_not(first))
     def _():
-        copy = pltpu.make_async_copy(whole_ref, c_hbm, sem)
-        copy.start()
-        copy.wait()
-
-
-def place_mine_kernel(tiles_ref, b_hbm, c_hbm, whole_ref, sem):
-    place(tiles_ref, whole_ref, b_hbm, c_hbm, lax.axis_index("core") == 0, sem)
-
-
-def place_other_kernel(tiles_ref, b_in, c_in, b_hbm, c_hbm, whole_ref, sem):
-    place(tiles_ref, whole_ref, b_hbm, c_hbm, lax.axis_index("core") == 1, sem)
+        write(other_ref, b_ref)
+        write(mine_ref, c_ref)
 
 
 def shape(*dims, dtype=F32):
@@ -325,11 +326,11 @@
         compiler_params=PARAMS,
     )(block_order, got)
     back = exchange(carried, SEQ)
-    came, keep, give = pl.pallas_call(
+    came, own_side, give = pl.pallas_call(
         grads_kernel,
         out_shape=(
             shape(state, inner, dtype=BF16),
-            shape(state // 8 * tile_cols, 8, 128),
+            shape(rows, state, dtype=BF16),
             shape(state // 8 * tile_cols, 8, 128),
         ),
         in_specs=[VMEM] * 7,
@@ -339,6 +340,14 @@
         cost_estimate=cost,
     )(layer_in, back, pushed, seen, mats, scores, enter)
     given = swap_cores(give)
+    keep = pl.pallas_call(
+        functools.partial(keep_kernel, 1.0 / (rows * blocks * lax.axis_size(DP))),
+        out_shape=shape(state // 8 * tile_cols, 8, 128),
+        in_specs=[VMEM] * 2,
+        out_specs=VMEM,
+        compiler_params=PARAMS,
+        cost_estimate=cost,
+    )(layer_in, own_side)
     scan_out = pl.pallas_call(
         output_kernel,
         out_shape=shape(1, rows, inner, dtype=BF16),
@@ -353,26 +362,13 @@
     share = jnp.sum(everywhere(share, "z"), axis=0)
     mine = everywhere(share, SEQ).reshape(local.shape)
     other = swap_cores(mine)
-    halves = (shape(state, width_in), shape(state, width_in))
-    scratch = [pltpu.VMEM((state, width_in), F32), pltpu.SemaphoreType.DMA]
-    partly = pl.pallas_call(
-        place_mine_kernel,
-        out_shape=halves,
-        in_specs=[VMEM],
-        out_specs=(HBM, HBM),
-        scratch_shapes=scratch,
-        compiler_params=PARAMS,
-        cost_estimate=cost,
-    )(mine)
     b_grad, c_grad = pl.pallas_call(
-        place_other_kernel,
-        out_shape=halves,
-        in_specs=[VMEM, HBM, HBM],
-        out_specs=(HBM, HBM),
-        scratch_shapes=scratch,
-        input_output_aliases={1: 0, 2: 1},
-        compiler_params=PARAMS,
-    )(other, *partly)
+        unpack_kernel,
+        out_shape=(shape(state, width_in), shape(state, width_in)),
+        in_specs=[VMEM] * 2,
+        out_specs=(VMEM,) * 2,
+        compiler_params=PARAMS,
+    )(mine, other)
     return scan_out, b_grad.T, c_grad.T
 
 

time: 116 us -> 115 us (level)
  transfers between devices with their start and end apart: 2 -> 2, of which waited for: 1 -> 2; matrix products, arithmetic and copies ran while one was open for 0% -> 0% of each run, Pallas kernels for 2% -> 2%
where the time goes in v4:
time: 115 us
  blocking collectives  96.9 us (84%)
  Pallas kernels  9.01 us (8%)
  starting transfers between devices  6.46 us (6%)
  waiting for transfers between devices  1.66 us (1%)
    all_to_all x5, blocking collectives, exchange(): return lax.all_to_all(a, axes, 0, 0, tiled=True)  96.9 us
    ppermute x2, starting transfers between devices, swap_cores(): return lax.ppermute(a, 'core', [(0, 1), (1, 0)])  6.46 us
    pallas_call x1, Pallas kernels, device_step(): pl.pallas_call(states_kernel, out_shape=tuple((shape(*dims, dtype=dtype)...  4.14 us
  transfers between devices with their start and end apart: 2, of which 2 were waited for; matrix products, arithmetic and copies ran while one was open for 0% of the time, Pallas kernels for 2%

profile of v4, /device:TPU:1, one launch (start us, length us, event | category | flops | bytes accessed | tf_op | source)
XLA Modules:
  0.0 115.1 jit_solution(4025612007614211803)
XLA Ops:
  0.6 4.1 %shard_map.121 = (f32[16,8,2688]{2,1,0:T(8,128)}, bf16[128,2560]{1,0:T(8,128)(2,1)}, bf16[128,2560]{1,0:T(8,128)(2,1)}, bf16[5,128,64]{2,1,0:T(8,128)(2,1)}, bf1...) custom-call(s32[1,4]{1,0:T(1,128)} %lengths_hbm.1, s32[1,16]{1,0:T(1,128)} %order_ref.1, bf16[1,128,2560]{2,1,0:T(8,128)(2,1)} %layer_ref.3, ...), custom_call_target="tpu_custom_call" | custom-call | tf_op jit(solution)/shard_map/pallas_call | solution.py:295
  4.8 0.0 copy-start.2
  4.8 27.4 %all_to_all.25.got_ref = f32[16,8,2688]{2,1,0:T(8,128)S(1)} all-to-all(f32[16,8,2688]{2,1,0:T(8,128)} %get-tuple-element.14), channel_id=1, replica_groups=mesh['z'=8,'core'=2,'y'=4,'x'=4] {'y','x'}, dimensions={0} | all-to-all | bytes 2752512 | tf_op jit(solution)/shard_map/all_to_all | solution.py:270
  32.2 0.0 copy-done.2
  32.2 0.8 shard_map.122
  33.1 0.0 copy-start
  33.1 0.0 copy-start.3
  33.1 0.0 copy-start.4
  33.1 0.0 copy-start.5
  33.1 0.0 copy-start.6
  33.1 0.0 copy-start.7
  33.1 21.6 %all_to_all.26.got_ref = f32[16,8,2560]{2,1,0:T(8,128)S(1)} all-to-all(f32[16,8,2560]{2,1,0:T(8,128)S(1)} %shard_map.122), channel_id=1, replica_groups=mesh['z'=8,'core'=2,'y'=4,'x'=4] {'y','x'}, dimensions={0} | all-to-all | bytes 2621440 | tf_op jit(solution)/shard_map/all_to_all | solution.py:270
  54.7 0.0 copy-done
  54.7 0.0 copy-done.3
  54.7 0.0 copy-done.4
  54.7 0.0 copy-done.5
  54.7 0.0 copy-done.6
  54.8 0.0 copy-done.7
  54.8 1.1 shard_map.123
  55.9 2.6 %collective-permute-start = (f32[160,8,128]{2,1,0:T(8,128)S(1)}, f32[160,8,128]{2,1,0:T(8,128)S(1)}, u32[]{:S(2)}, u32[]{:S(2)}) collective-permute-start(f32[160,8,128]{2,1,0:T(8,128)S(1)} %get-tuple-element.22), channel_id=1, source_target_pairs={{0,16},{16,0},{1,17},{17,1},{2,18},{18,2},{3,19},{19,3},{4,20},{20... | collective-permute-start | bytes 1966088 | tf_op jit(solution)/shard_map/ppermute | solution.py:266
  58.5 0.3 shard_map.125
  58.8 1.4 %collective-permute-done = f32[160,8,128]{2,1,0:T(8,128)S(1)} collective-permute-done((f32[160,8,128]{2,1,0:T(8,128)S(1)}, f32[160,8,128]{2,1,0:T(8,128)S(1)}, u32[]{:S(2)}, u32[]{:S(2)}) %collective-permute-start) | collective-permute-done | bytes 655392 | tf_op jit(solution)/shard_map/ppermute | solution.py:266
  60.2 0.1 add.3
  60.3 15.1 %all_to_all.27 = f32[16,10,8,128]{3,2,1,0:T(8,128)S(1)} all-to-all(f32[16,10,8,128]{3,2,1,0:T(8,128)S(1)} %bitcast.12), channel_id=1, replica_groups=mesh['z'=8,'core'=2,'y'=4,'x'=4] {'y','x'}, dimensions={0} | all-to-all | bytes 1310720 | tf_op jit(solution)/shard_map/all_to_all | solution.py:270
  75.5 0.0 copy-start.1
  75.5 0.0 copy-start.8
  75.5 18.9 %all_to_all.28 = f32[8,10,8,128]{3,2,1,0:T(8,128)S(1)} all-to-all(f32[8,10,8,128]{3,2,1,0:T(8,128)S(1)} %broadcast_in_dim.20), channel_id=1, replica_groups=mesh['z'=8,'core'=2,'y'=4,'x'=4] {'z'}, dimensions={0} | all-to-all | bytes 655360 | tf_op jit(solution)/shard_map/all_to_all | solution.py:270
  94.5 13.9 %all_to_all.29 = f32[16,10,8,128]{3,2,1,0:T(8,128)S(1)} all-to-all(f32[16,10,8,128]{3,2,1,0:T(8,128)S(1)} %broadcast_in_dim.21), channel_id=1, replica_groups=mesh['z'=8,'core'=2,'y'=4,'x'=4] {'y','x'}, dimensions={0} | all-to-all | bytes 1310720 | tf_op jit(solution)/shard_map/all_to_all | solution.py:270
  108.4 3.8 %collective-permute-start.1 = (f32[160,8,128]{2,1,0:T(8,128)S(1)}, f32[160,8,128]{2,1,0:T(8,128)S(1)}, u32[]{:S(2)}, u32[]{:S(2)}) collective-permute-start(f32[160,8,128]{2,1,0:T(8,128)S(1)} %bitcast.9), channel_id=1, source_target_pairs={{0,16},{16,0},{1,17},{17,1},{2,18},{18,2},{3,19},{19,3},{4,20},{20... | collective-permute-start | bytes 1966088 | tf_op jit(solution)/shard_map/ppermute | solution.py:266
  112.2 0.0 copy-done.1
  112.2 0.0 copy-done.8
  112.2 1.5 %shard_map.124 = bf16[1,128,2560]{2,1,0:T(8,128)(2,1)} custom-call(bf16[1,128,2560]{2,1,0:T(8,128)(2,1)S(1)} %copy-done.1, f32[1,40]{1,0:T(1,128)S(1)} %bitcast.11, bf16[64,2560]{1,0:T(8,128)(2,1)S(1)} %get-tuple-element.20.came_ref, bf16[128,2560]{1,0:T(8,128)(2,1)S(1)} %copy-done.3, bf16[2,128,128]{2,1,0:T(8,128)(2,1)S(1)} %copy-done.6, ...), custom_call_target="tpu_custom_call" | custom-call | flops 1000000000 | bytes 1000000 | tf_op jit(solution)/shard_map/pallas_call | solution.py:351
  113.7 0.2 collective-permute-done.1.other_ref
  113.9 1.1 shard_map.126
  (4 shorter events, 0.1 us)
Async XLA Ops:
  4.8 27.4 %copy-start.2 = (s32[1,16]{1,0:T(1,128)S(1)}, s32[1,16]{1,0:T(1,128)}, u32[]{:S(2)}) copy-start(s32[1,16]{1,0:T(1,128)} %order_ref.1) | copy-start | bytes 196
  33.1 21.7 %copy-start = (bf16[1,128,2560]{2,1,0:T(8,128)(2,1)S(1)}, bf16[1,128,2560]{2,1,0:T(8,128)(2,1)}, u32[]{:S(2)}) copy-start(bf16[1,128,2560]{2,1,0:T(8,128)(2,1)} %layer_ref.3) | copy-start | bytes 1966084
  33.1 21.6 %copy-start.3 = (bf16[128,2560]{1,0:T(8,128)(2,1)S(1)}, bf16[128,2560]{1,0:T(8,128)(2,1)}, u32[]{:S(2)}) copy-start(bf16[128,2560]{1,0:T(8,128)(2,1)} %get-tuple-element.15.pushed_ref) | copy-start | bytes 1966084
  33.1 21.6 %copy-start.4 = (bf16[128,2560]{1,0:T(8,128)(2,1)S(1)}, bf16[128,2560]{1,0:T(8,128)(2,1)}, u32[]{:S(2)}) copy-start(bf16[128,2560]{1,0:T(8,128)(2,1)} %get-tuple-element.16.seen_ref) | copy-start | bytes 1966084
  33.1 21.6 %copy-start.5 = (bf16[5,128,64]{2,1,0:T(8,128)(2,1)S(1)}, bf16[5,128,64]{2,1,0:T(8,128)(2,1)}, u32[]{:S(2)}) copy-start(bf16[5,128,64]{2,1,0:T(8,128)(2,1)} %get-tuple-element.17.mats_ref) | copy-start | bytes 245764
  33.1 21.6 %copy-start.6 = (bf16[2,128,128]{2,1,0:T(8,128)(2,1)S(1)}, bf16[2,128,128]{2,1,0:T(8,128)(2,1)}, u32[]{:S(2)}) copy-start(bf16[2,128,128]{2,1,0:T(8,128)(2,1)} %get-tuple-element.18.scores_ref) | copy-start | bytes 196612
  33.1 21.6 %copy-start.7 = (f32[128,128]{1,0:T(8,128)S(1)}, f32[128,128]{1,0:T(8,128)}, u32[]{:S(2)}) copy-start(f32[128,128]{1,0:T(8,128)} %get-tuple-element.19.enter_ref) | copy-start | bytes 196612
  55.9 4.4 %collective-permute-start = (f32[160,8,128]{2,1,0:T(8,128)S(1)}, f32[160,8,128]{2,1,0:T(8,128)S(1)}, u32[]{:S(2)}, u32[]{:S(2)}) collective-permute-start(f32[160,8,128]{2,1,0:T(8,128)S(1)} %get-tuple-element.22), channel_id=1, source_target_pairs={{0,16},{16,0},{1,17},{17,1},{2,18},{18,2},{3,19},{19,3},{4,20},{20... | collective-permute-start | bytes 1966088 | tf_op jit(solution)/shard_map/ppermute | solution.py:266
  75.5 36.7 %copy-start.1 = (bf16[1,128,2560]{2,1,0:T(8,128)(2,1)S(1)}, bf16[1,128,2560]{2,1,0:T(8,128)(2,1)}, u32[]{:S(2)}) copy-start(bf16[1,128,2560]{2,1,0:T(8,128)(2,1)} %x_ref.1) | copy-start | bytes 1966084
  75.5 36.7 %copy-start.8 = (f32[40]{0:T(128)S(1)}, f32[40]{0:T(128)}, u32[]{:S(2)}) copy-start(f32[40]{0:T(128)} %param.16) | copy-start | bytes 484
  108.4 5.6 %collective-permute-start.1 = (f32[160,8,128]{2,1,0:T(8,128)S(1)}, f32[160,8,128]{2,1,0:T(8,128)S(1)}, u32[]{:S(2)}, u32[]{:S(2)}) collective-permute-start(f32[160,8,128]{2,1,0:T(8,128)S(1)} %bitcast.9), channel_id=1, source_target_pairs={{0,16},{16,0},{1,17},{17,1},{2,18},{18,2},{3,19},{19,3},{4,20},{20... | collective-permute-start | bytes 1966088 | tf_op jit(solution)/shard_map/ppermute | solution.py:266

commit v5 on v4

--- a/solution.py
+++ b/solution.py
@@ -16,6 +16,7 @@
 CHUNK = 256
 EXTRA = 128
 OUT = 512
+PIECES = 2
 
 
 VMEM = pl.BlockSpec(memory_space=pltpu.VMEM)
@@ -237,25 +238,36 @@
         out_ref[0, :, cols] = (spread(enter, h, per, width) * mixed + skip).astype(BF16)
 
 
-def unpack_kernel(mine_ref, other_ref, b_ref, c_ref):
-    columns = b_ref.shape[1] // 128
-
-    def write(from_ref, to_ref):
-        for r in range(to_ref.shape[0] // 8):
-            for c in range(columns):
-                to_ref[8 * r : 8 * r + 8, 128 * c : 128 * c + 128] = from_ref[r * columns + c]
-
-    first = lax.axis_index("core") == 0
-
-    @pl.when(first)
+def unpack_kernel(mine_ref, other_ref, b_hbm, c_hbm, mine_whole, other_whole, sems):
+    state, width = mine_whole.shape
+    columns = width // 128
+    piece = state // PIECES
+    low = lax.axis_index("core") == 0
+    to_low, to_high = [], []
+    for side, (from_ref, whole) in enumerate(((mine_ref, mine_whole), (other_ref, other_whole))):
+        for p in range(PIECES):
+            for r in range(p * piece // 8, (p + 1) * piece // 8):
+                for c in range(columns):
+                    whole[8 * r : 8 * r + 8, 128 * c : 128 * c + 128] = from_ref[r * columns + c]
+            rows = slice(p * piece, (p + 1) * piece)
+            sem = sems.at[side * PIECES + p]
+            ends = (b_hbm, c_hbm) if side == 0 else (c_hbm, b_hbm)
+            first = pltpu.make_async_copy(whole.at[rows], ends[0].at[rows], sem)
+            second = pltpu.make_async_copy(whole.at[rows], ends[1].at[rows], sem)
+            pl.when(low)(first.start)
+            pl.when(jnp.logical_not(low))(second.start)
+            to_low.append(first)
+            to_high.append(second)
+
+    @pl.when(low)
     def _():
-        write(mine_ref, b_ref)
-        write(other_ref, c_ref)
-
-    @pl.when(jnp.logical_not(first))
+        for copy in to_low:
+            copy.wait()
+
+    @pl.when(jnp.logical_not(low))
     def _():
-        write(other_ref, b_ref)
-        write(mine_ref, c_ref)
+        for copy in to_high:
+            copy.wait()
 
 
 def shape(*dims, dtype=F32):
@@ -366,7 +378,12 @@
         unpack_kernel,
         out_shape=(shape(state, width_in), shape(state, width_in)),
         in_specs=[VMEM] * 2,
-        out_specs=(VMEM,) * 2,
+        out_specs=(HBM,) * 2,
+        scratch_shapes=[
+            pltpu.VMEM((state, width_in), F32),
+            pltpu.VMEM((state, width_in), F32),
+            pltpu.SemaphoreType.DMA((2 * PIECES,)),
+        ],
         compiler_params=PARAMS,
     )(mine, other)
     return scan_out, b_grad.T, c_grad.T

time: 115 us -> 115 us (level)
  no operation moved by 1% of the time
where the time goes in v5:
time: 115 us
  blocking collectives  96.9 us (84%)
  Pallas kernels  8.97 us (8%)
  starting transfers between devices  6.46 us (6%)
  waiting for transfers between devices  1.66 us (1%)
    all_to_all x5, blocking collectives, exchange(): return lax.all_to_all(a, axes, 0, 0, tiled=True)  96.9 us
    ppermute x2, starting transfers between devices, swap_cores(): return lax.ppermute(a, 'core', [(0, 1), (1, 0)])  6.46 us
    pallas_call x1, Pallas kernels, device_step(): pl.pallas_call(states_kernel, out_shape=tuple((shape(*dims, dtype=dtype)...  4.14 us
  transfers between devices with their start and end apart: 2, of which 2 were waited for; matrix products, arithmetic and copies ran while one was open for 0% of the time, Pallas kernels for 2%

profile of v5, /device:TPU:1, one launch (start us, length us, event | category | flops | bytes accessed | tf_op | source)
XLA Modules:
  0.0 115.0 jit_solution(7961698868346296971)
XLA Ops:
  0.6 4.1 %shard_map.121 = (f32[16,8,2688]{2,1,0:T(8,128)}, bf16[128,2560]{1,0:T(8,128)(2,1)}, bf16[128,2560]{1,0:T(8,128)(2,1)}, bf16[5,128,64]{2,1,0:T(8,128)(2,1)}, bf1...) custom-call(s32[1,4]{1,0:T(1,128)} %lengths_hbm.1, s32[1,16]{1,0:T(1,128)} %order_ref.1, bf16[1,128,2560]{2,1,0:T(8,128)(2,1)} %layer_ref.3, ...), custom_call_target="tpu_custom_call" | custom-call | tf_op jit(solution)/shard_map/pallas_call | solution.py:307
  4.8 0.0 copy-start.2
  4.8 27.4 %all_to_all.25.got_ref = f32[16,8,2688]{2,1,0:T(8,128)S(1)} all-to-all(f32[16,8,2688]{2,1,0:T(8,128)} %get-tuple-element.14), channel_id=1, replica_groups=mesh['z'=8,'core'=2,'y'=4,'x'=4] {'y','x'}, dimensions={0} | all-to-all | bytes 2752512 | tf_op jit(solution)/shard_map/all_to_all | solution.py:282
  32.2 0.0 copy-done.2
  32.2 0.8 shard_map.122
  33.1 0.0 copy-start
  33.1 0.0 copy-start.3
  33.1 0.0 copy-start.4
  33.1 0.0 copy-start.5
  33.1 0.0 copy-start.6
  33.1 0.0 copy-start.7
  33.1 21.6 %all_to_all.26.got_ref = f32[16,8,2560]{2,1,0:T(8,128)S(1)} all-to-all(f32[16,8,2560]{2,1,0:T(8,128)S(1)} %shard_map.122), channel_id=1, replica_groups=mesh['z'=8,'core'=2,'y'=4,'x'=4] {'y','x'}, dimensions={0} | all-to-all | bytes 2621440 | tf_op jit(solution)/shard_map/all_to_all | solution.py:282
  54.7 0.0 copy-done
  54.7 0.0 copy-done.3
  54.7 0.0 copy-done.4
  54.7 0.0 copy-done.5
  54.7 0.0 copy-done.6
  54.8 0.0 copy-done.7
  54.8 1.1 shard_map.123
  55.9 2.6 %collective-permute-start = (f32[160,8,128]{2,1,0:T(8,128)S(1)}, f32[160,8,128]{2,1,0:T(8,128)S(1)}, u32[]{:S(2)}, u32[]{:S(2)}) collective-permute-start(f32[160,8,128]{2,1,0:T(8,128)S(1)} %get-tuple-element.22), channel_id=1, source_target_pairs={{0,16},{16,0},{1,17},{17,1},{2,18},{18,2},{3,19},{19,3},{4,20},{20... | collective-permute-start | bytes 1966088 | tf_op jit(solution)/shard_map/ppermute | solution.py:278
  58.5 0.3 shard_map.125
  58.8 1.4 %collective-permute-done = f32[160,8,128]{2,1,0:T(8,128)S(1)} collective-permute-done((f32[160,8,128]{2,1,0:T(8,128)S(1)}, f32[160,8,128]{2,1,0:T(8,128)S(1)}, u32[]{:S(2)}, u32[]{:S(2)}) %collective-permute-start) | collective-permute-done | bytes 655392 | tf_op jit(solution)/shard_map/ppermute | solution.py:278
  60.2 0.1 add.3
  60.3 15.1 %all_to_all.27 = f32[16,10,8,128]{3,2,1,0:T(8,128)S(1)} all-to-all(f32[16,10,8,128]{3,2,1,0:T(8,128)S(1)} %bitcast.12), channel_id=1, replica_groups=mesh['z'=8,'core'=2,'y'=4,'x'=4] {'y','x'}, dimensions={0} | all-to-all | bytes 1310720 | tf_op jit(solution)/shard_map/all_to_all | solution.py:282
  75.5 0.0 copy-start.1
  75.5 0.0 copy-start.8
  75.5 18.9 %all_to_all.28 = f32[8,10,8,128]{3,2,1,0:T(8,128)S(1)} all-to-all(f32[8,10,8,128]{3,2,1,0:T(8,128)S(1)} %broadcast_in_dim.20), channel_id=1, replica_groups=mesh['z'=8,'core'=2,'y'=4,'x'=4] {'z'}, dimensions={0} | all-to-all | bytes 655360 | tf_op jit(solution)/shard_map/all_to_all | solution.py:282
  94.5 13.9 %all_to_all.29 = f32[16,10,8,128]{3,2,1,0:T(8,128)S(1)} all-to-all(f32[16,10,8,128]{3,2,1,0:T(8,128)S(1)} %broadcast_in_dim.21), channel_id=1, replica_groups=mesh['z'=8,'core'=2,'y'=4,'x'=4] {'y','x'}, dimensions={0} | all-to-all | bytes 1310720 | tf_op jit(solution)/shard_map/all_to_all | solution.py:282
  108.4 3.8 %collective-permute-start.1 = (f32[160,8,128]{2,1,0:T(8,128)S(1)}, f32[160,8,128]{2,1,0:T(8,128)S(1)}, u32[]{:S(2)}, u32[]{:S(2)}) collective-permute-start(f32[160,8,128]{2,1,0:T(8,128)S(1)} %bitcast.9), channel_id=1, source_target_pairs={{0,16},{16,0},{1,17},{17,1},{2,18},{18,2},{3,19},{19,3},{4,20},{20... | collective-permute-start | bytes 1966088 | tf_op jit(solution)/shard_map/ppermute | solution.py:278
  112.2 0.0 copy-done.1
  112.2 0.0 copy-done.8
  112.2 1.5 %shard_map.124 = bf16[1,128,2560]{2,1,0:T(8,128)(2,1)} custom-call(bf16[1,128,2560]{2,1,0:T(8,128)(2,1)S(1)} %copy-done.1, f32[1,40]{1,0:T(1,128)S(1)} %bitcast.11, bf16[64,2560]{1,0:T(8,128)(2,1)S(1)} %get-tuple-element.20.came_ref, bf16[128,2560]{1,0:T(8,128)(2,1)S(1)} %copy-done.3, bf16[2,128,128]{2,1,0:T(8,128)(2,1)S(1)} %copy-done.6, ...), custom_call_target="tpu_custom_call" | custom-call | flops 1000000000 | bytes 1000000 | tf_op jit(solution)/shard_map/pallas_call | solution.py:363
  113.7 0.2 collective-permute-done.1.other_ref
  113.9 1.1 shard_map.126
  (4 shorter events, 0.1 us)
Async XLA Ops:
  4.8 27.4 %copy-start.2 = (s32[1,16]{1,0:T(1,128)S(1)}, s32[1,16]{1,0:T(1,128)}, u32[]{:S(2)}) copy-start(s32[1,16]{1,0:T(1,128)} %order_ref.1) | copy-start | bytes 196
  33.1 21.7 %copy-start = (bf16[1,128,2560]{2,1,0:T(8,128)(2,1)S(1)}, bf16[1,128,2560]{2,1,0:T(8,128)(2,1)}, u32[]{:S(2)}) copy-start(bf16[1,128,2560]{2,1,0:T(8,128)(2,1)} %layer_ref.3) | copy-start | bytes 1966084
  33.1 21.6 %copy-start.3 = (bf16[128,2560]{1,0:T(8,128)(2,1)S(1)}, bf16[128,2560]{1,0:T(8,128)(2,1)}, u32[]{:S(2)}) copy-start(bf16[128,2560]{1,0:T(8,128)(2,1)} %get-tuple-element.15.pushed_ref) | copy-start | bytes 1966084
  33.1 21.6 %copy-start.4 = (bf16[128,2560]{1,0:T(8,128)(2,1)S(1)}, bf16[128,2560]{1,0:T(8,128)(2,1)}, u32[]{:S(2)}) copy-start(bf16[128,2560]{1,0:T(8,128)(2,1)} %get-tuple-element.16.seen_ref) | copy-start | bytes 1966084
  33.1 21.6 %copy-start.5 = (bf16[5,128,64]{2,1,0:T(8,128)(2,1)S(1)}, bf16[5,128,64]{2,1,0:T(8,128)(2,1)}, u32[]{:S(2)}) copy-start(bf16[5,128,64]{2,1,0:T(8,128)(2,1)} %get-tuple-element.17.mats_ref) | copy-start | bytes 245764
  33.1 21.6 %copy-start.6 = (bf16[2,128,128]{2,1,0:T(8,128)(2,1)S(1)}, bf16[2,128,128]{2,1,0:T(8,128)(2,1)}, u32[]{:S(2)}) copy-start(bf16[2,128,128]{2,1,0:T(8,128)(2,1)} %get-tuple-element.18.scores_ref) | copy-start | bytes 196612
  33.1 21.6 %copy-start.7 = (f32[128,128]{1,0:T(8,128)S(1)}, f32[128,128]{1,0:T(8,128)}, u32[]{:S(2)}) copy-start(f32[128,128]{1,0:T(8,128)} %get-tuple-element.19.enter_ref) | copy-start | bytes 196612
  55.9 4.4 %collective-permute-start = (f32[160,8,128]{2,1,0:T(8,128)S(1)}, f32[160,8,128]{2,1,0:T(8,128)S(1)}, u32[]{:S(2)}, u32[]{:S(2)}) collective-permute-start(f32[160,8,128]{2,1,0:T(8,128)S(1)} %get-tuple-element.22), channel_id=1, source_target_pairs={{0,16},{16,0},{1,17},{17,1},{2,18},{18,2},{3,19},{19,3},{4,20},{20... | collective-permute-start | bytes 1966088 | tf_op jit(solution)/shard_map/ppermute | solution.py:278
  75.5 36.7 %copy-start.1 = (bf16[1,128,2560]{2,1,0:T(8,128)(2,1)S(1)}, bf16[1,128,2560]{2,1,0:T(8,128)(2,1)}, u32[]{:S(2)}) copy-start(bf16[1,128,2560]{2,1,0:T(8,128)(2,1)} %x_ref.1) | copy-start | bytes 1966084
  75.5 36.7 %copy-start.8 = (f32[40]{0:T(128)S(1)}, f32[40]{0:T(128)}, u32[]{:S(2)}) copy-start(f32[40]{0:T(128)} %param.16) | copy-start | bytes 484
  108.4 5.6 %collective-permute-start.1 = (f32[160,8,128]{2,1,0:T(8,128)S(1)}, f32[160,8,128]{2,1,0:T(8,128)S(1)}, u32[]{:S(2)}, u32[]{:S(2)}) collective-permute-start(f32[160,8,128]{2,1,0:T(8,128)S(1)} %bitcast.9), channel_id=1, source_target_pairs={{0,16},{16,0},{1,17},{17,1},{2,18},{18,2},{3,19},{19,3},{4,20},{20... | collective-permute-start | bytes 1966088 | tf_op jit(solution)/shard_map/ppermute | solution.py:278
